TPU v7x, 32 devices: a whole 2x2x4 slice. The times are simulated.
32 devices in a mesh: ta: 8 (over y, x, core), gz: 4 (over z).
Axes of the slice: x: 2, y: 2, z: 4, core: 2. Of those that a mesh axis runs over, the one named last changes fastest.
Arguments:
- spinor: float32 [2, 4, 3, 16, 8, 768], P(None, None, None, 'ta', 'gz'), may hold values from -3 to 3
- links: float32 [4, 2, 3, 3, 16, 8, 768], P(None, None, None, None, 'ta', 'gz'), may hold values from -3.5 to 3.5
- clover: float32 [2, 2, 6, 6, 16, 8, 768], P(None, None, None, None, 'ta', 'gz'), may hold values from -1.2 to 1.2
Outputs:
- applied: float32 [2, 4, 3, 16, 8, 768], P(None, None, None, 'ta', 'gz')
- force: float32 [4, 2, 3, 3, 16, 8, 768], P(None, None, None, None, 'ta', 'gz')
All inputs are finite; a program needn't handle non-finite values.
Results may differ from a plain program's by a relative error of at most 0.0001.
Values sent between devices are 32-bit elements; how exact they have to be, the bound alone decides.
A program may use at most 64 MiB of HBM per device.

v0:
```python
import jax
import jax.numpy as jnp
from jax import lax
from jax.experimental import pallas as pl
from jax.experimental.pallas import tpu as pltpu
from jax.sharding import PartitionSpec as P

NX = 64
LANES = 128
TILE = 8
MESH = pl.DeviceIdType.MESH

bare_mass = -0.25
gamma_table = (
    ((3, 0.0, -1.0), (2, 0.0, -1.0), (1, 0.0, 1.0), (0, 0.0, 1.0)),
    ((3, -1.0, 0.0), (2, 1.0, 0.0), (1, 1.0, 0.0), (0, -1.0, 0.0)),
    ((2, 0.0, -1.0), (3, 0.0, 1.0), (0, 0.0, 1.0), (1, 0.0, -1.0)),
    ((2, 1.0, 0.0), (3, 1.0, 0.0), (0, 1.0, 0.0), (1, 1.0, 0.0)),
)


def add_signed(a, b, positive):
    return a + b if positive else a - b


def add_phase(a, b, phase_re, phase_im):
    if phase_im == 0.0:
        up = phase_re > 0
        return (add_signed(a[0], b[0], up), add_signed(a[1], b[1], up))
    up = phase_im > 0
    return (add_signed(a[0], b[1], not up), add_signed(a[1], b[0], up))


def half(mu, field, sign):
    out = []
    for s in range(2):
        source, p_re, p_im = gamma_table[mu][s]
        out.append(
            [add_phase(field[s][c], field[source][c], sign * p_re, sign * p_im) for c in range(3)]
        )
    return out


def add_whole(mu, total, halves, sign):
    out = [[add_phase(total[s][c], halves[s][c], 1.0, 0.0) for c in range(3)] for s in range(2)]
    for s in (2, 3):
        source, p_re, p_im = gamma_table[mu][s]
        out.append(
            [add_phase(total[s][c], halves[source][c], sign * p_re, sign * p_im) for c in range(3)]
        )
    return out


def csum(terms):
    total = terms[0]
    for term in terms[1:]:
        total = total + term
    return total


def mat_vec(link, vec, dagger):
    out = []
    for s in range(2):
        rows = []
        for a in range(3):
            re, im = [], []
            for b in range(3):
                h = vec[s][b]
                if dagger:
                    m = link[b][a]
                    re.append(m[0] * h[0] + m[1] * h[1])
                    im.append(m[0] * h[1] - m[1] * h[0])
                else:
                    m = link[a][b]
                    re.append(m[0] * h[0] - m[1] * h[1])
                    im.append(m[0] * h[1] + m[1] * h[0])
            rows.append((csum(re), csum(im)))
        out.append(rows)
    return out


def flat(ref):
    return ref.reshape(ref.shape[0], ref.shape[1] * ref.shape[2], ref.shape[3])


def parts_of(whole, held):
    parts = whole.shape[-1] // LANES
    for t in range(whole.shape[-3]):
        for q in range(parts):
            yield whole.at[:, t, :, pl.ds(LANES * q, LANES)], held.at[:, parts * t + q]


def write_out(phi_ref, force_ref, out_hbm, force_hbm, sem):
    for n, (whole, held) in enumerate(((force_hbm, force_ref), (out_hbm, phi_ref))):
        for dst, src in parts_of(whole, held):
            pltpu.make_async_copy(src, dst, sem.at[n]).start()
    for n, held in enumerate((force_ref, phi_ref)):
        pltpu.make_async_copy(held, held, sem.at[n]).wait()


def kernel(nt, nz, x_hbm, u_hbm, c_hbm, phi_out, force_out, psi_in, link_in, clov_in, hm, hp, bl,
           sh_hm, sh_bl, prod, acc, hphi, sh_hphi, face_out, face_in, in_sem, send_sem, recv_sem):
    psi, link, clov, out_ref, force_ref = map(flat, (psi_in, link_in, clov_in, phi_out, force_out))
    rows = psi.shape[1]
    face_t = rows // nt
    face_z = rows // nz
    chunks = rows // TILE
    t_place, z_place = lax.axis_index("ta"), lax.axis_index("gz")
    t_count, z_count = lax.axis_size("ta"), lax.axis_size("gz")
    t_next = (lax.rem(t_place + 1, t_count), z_place)
    t_prev = (lax.rem(t_place + t_count - 1, t_count), z_place)
    z_next = (t_place, lax.rem(z_place + 1, z_count))
    z_prev = (t_place, lax.rem(z_place + z_count - 1, z_count))
    low_sign = jnp.where(t_place == 0, -1.0, 1.0).astype(jnp.float32)
    high_sign = jnp.where(t_place == t_count - 1, -1.0, 1.0).astype(jnp.float32)

    barrier = pltpu.get_barrier_semaphore()
    for target in (t_next, t_prev, z_next, z_prev):
        pl.semaphore_signal(barrier, inc=1, device_id=target, device_id_type=MESH)

    groups = [(x_hbm, psi_in)]
    for mu in range(4):
        part = pl.ds(18 * mu, 18)
        groups.append((u_hbm.at[part], link_in.at[part]))
    groups.append((c_hbm, clov_in))
    for n in (0, 3, 4, 1, 2, 5):
        for src, dst in parts_of(*groups[n]):
            pltpu.make_async_copy(src, dst, in_sem.at[n]).start()

    def arrived(n):
        held = groups[n][1]
        pltpu.make_async_copy(held, held, in_sem.at[n]).wait()

    def window(v):
        return pl.ds(pl.multiple_of(v * TILE, TILE), TILE)

    def load_spinor(ref, at):
        return [[(ref[3 * s + c, at, :], ref[12 + 3 * s + c, at, :]) for c in range(3)] for s in range(4)]

    def load_half(ref, mu, at):
        return [[(ref[mu, 3 * s + c, at, :], ref[mu, 6 + 3 * s + c, at, :]) for c in range(3)] for s in range(2)]

    def store_half(ref, mu, at, value):
        for s in range(2):
            for c in range(3):
                ref[mu, 3 * s + c, at, :] = value[s][c][0]
                ref[mu, 6 + 3 * s + c, at, :] = value[s][c][1]

    def load_link(mu, at):
        return [[(link[18 * mu + 3 * a + b, at, :], link[18 * mu + 9 + 3 * a + b, at, :]) for b in range(3)] for a in range(3)]

    lane = lax.broadcasted_iota(jnp.int32, (rows, LANES), 1)
    row = lax.broadcasted_iota(jnp.int32, (rows, LANES), 0)
    lane_in = lax.rem(lane, NX)
    row_in = lax.rem(row, face_t)
    upper = lane >= NX

    def shift_x1(value, step):
        if step == 1:
            near, far = pltpu.roll(value, LANES - 1, 1), pltpu.roll(value, NX - 1, 1)
            return jnp.where(lane_in == NX - 1, far, near)
        near, far = pltpu.roll(value, 1, 1), pltpu.roll(value, LANES - NX + 1, 1)
        return jnp.where(lane_in == 0, far, near)

    def shift_x2(value, step):
        turned = pltpu.roll(value, NX, 1)
        if step == 1:
            near = pltpu.roll(turned, rows - nz, 0)
            far = pltpu.roll(turned, face_t - nz, 0)
            moved = jnp.where(row_in >= face_t - nz, far, near)
            return jnp.where(upper, moved, turned)
        near = pltpu.roll(turned, nz, 0)
        far = pltpu.roll(turned, rows - face_t + nz, 0)
        moved = jnp.where(row_in < nz, far, near)
        return jnp.where(upper, turned, moved)

    def z_ahead(src, dst, c):
        for z in range(nz - 1):
            dst[2, c, pl.ds(z, face_z, nz), :] = src[2, c, pl.ds(z + 1, face_z, nz), :]

    def z_behind(src, dst, c):
        for z in range(1, nz):
            dst[2, c, pl.ds(z, face_z, nz), :] = src[2, c, pl.ds(z - 1, face_z, nz), :]

    def t_ahead(src, dst, c):
        dst[3, c, pl.ds(0, rows - face_t), :] = src[3, c, pl.ds(face_t, rows - face_t), :]

    def t_behind(src, dst, c):
        dst[3, c, pl.ds(face_t, rows - face_t), :] = src[3, c, pl.ds(0, rows - face_t), :]

    def for_each(count, body):
        def step(i, carry):
            body(i)
            return carry

        lax.fori_loop(0, count, step, 0)

    targets = (t_prev, t_next, z_prev, z_next, t_prev, z_prev)
    sends = [
        pltpu.make_async_remote_copy(
            src_ref=face_out.at[k], dst_ref=face_in.at[k], send_sem=send_sem.at[k],
            recv_sem=recv_sem.at[k], device_id=targets[k], device_id_type=MESH,
        )
        for k in range(6)
    ]

    def project(mu, v):
        at = window(v)
        field = load_spinor(psi, at)
        store_half(hm, mu, at, half(mu, field, -1.0))
        ahead = half(mu, field, 1.0)
        store_half(hp, mu, at, ahead)
        store_half(bl, mu, at, mat_vec(load_link(mu, at), ahead, True))

    def face(k, c, size):
        return k, pl.ds(c * size, size)

    arrived(0)
    arrived(3)
    for_each(chunks, lambda v: project(2, v))
    for c in range(12):
        k, at = face(3, c, face_z)
        face_out[k, at, :] = bl[2, c, pl.ds(nz - 1, face_z, nz), :]
    pl.semaphore_wait(barrier, 4)
    sends[3].start()
    for c in range(12):
        k, at = face(2, c, face_z)
        face_out[k, at, :] = hm[2, c, pl.ds(0, face_z, nz), :]
    arrived(4)
    for_each(chunks, lambda v: project(3, v))
    for c in range(12):
        k, at = face(0, c, face_t)
        face_out[k, at, :] = hm[3, c, 0:face_t, :]
        k, at = face(1, c, face_t)
        face_out[k, at, :] = bl[3, c, rows - face_t:rows, :]
    sends[1].start()
    sends[0].start()
    sends[2].start()

    arrived(1)
    for_each(chunks, lambda v: project(0, v))
    arrived(2)
    for_each(chunks, lambda v: project(1, v))

    def shifts(c):
        sh_hm[0, c] = shift_x1(hm[0, c], 1)
        sh_bl[0, c] = shift_x1(bl[0, c], -1)
        sh_hm[1, c] = shift_x2(hm[1, c], 1)
        sh_bl[1, c] = shift_x2(bl[1, c], -1)
        z_ahead(hm, sh_hm, c)
        z_behind(bl, sh_bl, c)
        t_ahead(hm, sh_hm, c)
        t_behind(bl, sh_bl, c)

    for_each(12, shifts)

    def hop(mu, at, total):
        ahead = mat_vec(load_link(mu, at), load_half(sh_hm, mu, at), False)
        store_half(prod, mu, at, ahead)
        total = add_whole(mu, total, ahead, -1.0)
        return add_whole(mu, total, load_half(sh_bl, mu, at), 1.0)

    zero = jnp.zeros((TILE, LANES), jnp.float32)

    arrived(5)

    def local(v):
        at = window(v)
        field = load_spinor(psi, at)
        total = [[(zero, zero)] * 3 for _ in range(4)]
        for mu in (0, 1):
            total = hop(mu, at, total)
        for s in range(4):
            for c in range(3):
                base = 36 * (s // 2) + 6 * (3 * (s % 2) + c)
                re = (4.0 + bare_mass) * field[s][c][0] - 0.5 * total[s][c][0]
                im = (4.0 + bare_mass) * field[s][c][1] - 0.5 * total[s][c][1]
                for k in range(6):
                    other = field[2 * (s // 2) + k // 3][k % 3]
                    c_re = clov[base + k, at, :]
                    c_im = clov[72 + base + k, at, :]
                    re = re + (c_re * other[0] - c_im * other[1])
                    im = im + (c_re * other[1] + c_im * other[0])
                acc[3 * s + c, at, :] = re
                acc[12 + 3 * s + c, at, :] = im

    for_each(chunks, local)

    for k in (0, 1, 3):
        sends[k].wait_recv()
    for c in range(12):
        k, at = face(0, c, face_t)
        sh_hm[3, c, pl.ds(rows - face_t, face_t), :] = face_in[k, at, :] * high_sign
        k, at = face(1, c, face_t)
        sh_bl[3, c, pl.ds(0, face_t), :] = face_in[k, at, :] * low_sign
        k, at = face(3, c, face_z)
        sh_bl[2, c, pl.ds(0, face_z, nz), :] = face_in[k, at, :]
        sh_hm[2, c, pl.ds(nz - 1, face_z, nz), :] = jnp.zeros((face_z, LANES), jnp.float32)

    def finish(v, early):
        at = window(v)
        total = [[(zero, zero)] * 3 for _ in range(4)]
        for mu in (2, 3):
            total = hop(mu, at, total)
        held = load_spinor(acc, at)
        phi = [
            [(held[s][c][0] - 0.5 * total[s][c][0], held[s][c][1] - 0.5 * total[s][c][1]) for c in range(3)]
            for s in range(4)
        ]
        if early:
            store_half(hphi, 2, at, half(2, phi, 1.0))
            return
        for s in range(4):
            for c in range(3):
                out_ref[3 * s + c, at, :] = phi[s][c][0]
                out_ref[12 + 3 * s + c, at, :] = phi[s][c][1]
        for mu in range(4):
            store_half(hphi, mu, at, half(mu, phi, 1.0))

    for_each(chunks, lambda v: finish(v, True))
    for c in range(12):
        k, at = face(5, c, face_z)
        face_out[k, at, :] = hphi[2, c, pl.ds(0, face_z, nz), :]
    sends[5].start()

    sends[2].wait_recv()
    for c in range(12):
        k, at = face(2, c, face_z)
        sh_hm[2, c, pl.ds(nz - 1, face_z, nz), :] = face_in[k, at, :]
    for_each(chunks, lambda v: finish(v, False))
    for c in range(12):
        k, at = face(4, c, face_t)
        face_out[k, at, :] = hphi[3, c, 0:face_t, :]
    sends[4].start()

    def shifts_phi(c):
        sh_hphi[0, c] = shift_x1(hphi[0, c], 1)
        sh_hphi[1, c] = shift_x2(hphi[1, c], 1)
        z_ahead(hphi, sh_hphi, c)
        t_ahead(hphi, sh_hphi, c)

    for_each(12, shifts_phi)

    def force(mu, v):
        at = window(v)
        second = mat_vec(load_link(mu, at), load_half(sh_hphi, mu, at), False)
        second_right = load_half(hp, mu, at)
        first = load_half(prod, mu, at)
        first_right = half(mu, load_spinor(out_ref, at), -1.0)
        pairs = [(first[s], first_right[s]) for s in range(2)] + [(second[s], second_right[s]) for s in range(2)]

        def w_re(a, b):
            return csum([l[a][0] * r[b][0] + l[a][1] * r[b][1] for l, r in pairs])

        def w_im(a, b):
            return csum([l[a][1] * r[b][0] - l[a][0] * r[b][1] for l, r in pairs])

        diag = [w_im(a, a) for a in range(3)]
        third = (diag[0] + diag[1] + diag[2]) * (1.0 / 3.0)
        base = 18 * mu
        for a in range(3):
            force_ref[base + 4 * a, at, :] = zero
            force_ref[base + 9 + 4 * a, at, :] = diag[a] - third
            for b in range(a + 1, 3):
                re = 0.5 * (w_re(a, b) - w_re(b, a))
                im = 0.5 * (w_im(a, b) + w_im(b, a))
                force_ref[base + 3 * a + b, at, :] = re
                force_ref[base + 3 * b + a, at, :] = -re
                force_ref[base + 9 + 3 * a + b, at, :] = im
                force_ref[base + 9 + 3 * b + a, at, :] = im

    for mu in (0, 1):
        for_each(chunks, lambda v: force(mu, v))

    sends[4].wait_recv()
    for c in range(12):
        k, at = face(4, c, face_t)
        sh_hphi[3, c, pl.ds(rows - face_t, face_t), :] = face_in[k, at, :] * high_sign
    for_each(chunks, lambda v: force(3, v))
    sends[5].wait_recv()
    for c in range(12):
        k, at = face(5, c, face_z)
        sh_hphi[2, c, pl.ds(nz - 1, face_z, nz), :] = face_in[k, at, :]
    for_each(chunks, lambda v: force(2, v))
    for k in range(6):
        sends[k].wait_send()


def body(spinor, links, clover):
    nt, nz = spinor.shape[3], spinor.shape[4]
    sites = spinor.shape[-3:]
    x, u, c = (a.reshape((-1,) + sites) for a in (spinor, links, clover))
    parts = nt * (sites[2] // LANES)
    rows = parts * nz
    face = max(rows // nt, rows // nz)

    def halves():
        return pltpu.VMEM((4, 12, rows, LANES), jnp.float32)

    def held(array):
        return pltpu.VMEM((array.shape[0], parts, nz, LANES), jnp.float32)

    phi, anti = pl.pallas_call(
        lambda *refs: kernel(nt, nz, *refs),
        name="wilson",
        out_shape=(
            jax.ShapeDtypeStruct((24, parts, nz, LANES), jnp.float32),
            jax.ShapeDtypeStruct((u.shape[0], parts, nz, LANES), jnp.float32),
        ),
        in_specs=[pl.BlockSpec(memory_space=pl.ANY)] * 3,
        out_specs=(pl.BlockSpec(memory_space=pltpu.VMEM),) * 2,
        scratch_shapes=[
            held(x), held(u), held(c),
            halves(), halves(), halves(), halves(), halves(), halves(),
            pltpu.VMEM((24, rows, LANES), jnp.float32),
            halves(), halves(),
            pltpu.VMEM((6, 12 * face, LANES), jnp.float32),
            pltpu.VMEM((6, 12 * face, LANES), jnp.float32),
            pltpu.SemaphoreType.DMA((6,)),
            pltpu.SemaphoreType.DMA((6,)),
            pltpu.SemaphoreType.DMA((6,)),
        ],
        compiler_params=pltpu.CompilerParams(collective_id=0, has_side_effects=True),
    )(x, u, c)
    applied, force = pl.pallas_call(
        write_out,
        name="write_out",
        out_shape=(
            jax.ShapeDtypeStruct(x.shape, jnp.float32),
            jax.ShapeDtypeStruct(u.shape, jnp.float32),
        ),
        in_specs=[pl.BlockSpec(memory_space=pltpu.VMEM)] * 2,
        out_specs=(pl.BlockSpec(memory_space=pl.ANY),) * 2,
        scratch_shapes=[pltpu.SemaphoreType.DMA((2,))],
    )(phi, anti)
    return applied.reshape(spinor.shape), force.reshape(links.shape)


def solution(mesh):
    return jax.shard_map(
        body,
        mesh=mesh,
        in_specs=(
            P(None, None, None, "ta", "gz", None),
            P(None, None, None, None, "ta", "gz", None),
            P(None, None, None, None, "ta", "gz", None),
        ),
        out_specs=(
            P(None, None, None, "ta", "gz", None),
            P(None, None, None, None, "ta", "gz", None),
        ),
        check_vma=False,
    )
```

profile of v0, /device:TPU:1, one launch (start us, length us, event | category | flops | bytes accessed | tf_op | source)
XLA Modules:
  0.0 17.4 jit_solution(10142705448948518539)
XLA Ops:
  0.6 14.5 %wilson.1 = (f32[24,12,2,128]{3,2,1,0:T(2,128)}, f32[72,12,2,128]{3,2,1,0:T(2,128)}) custom-call(f32[24,2,2,768]{3,2,1,0:T(2,128)} %bitcast.7, f32[72,2,2,768]{3,2,1,0:T(2,128)} %bitcast.6, f32[144,2,2,768]{3,2,1,0:T(2,128)} %bitcast.5), custom_call_target="tpu_custom_call" | custom-call | tf_op jit(solution)/shard_map/wilson/pallas_call | solution.py:403
  15.2 2.3 %write_out.1 = (f32[24,2,2,768]{3,2,1,0:T(2,128)}, f32[72,2,2,768]{3,2,1,0:T(2,128)}) custom-call(f32[24,12,2,128]{3,2,1,0:T(2,128)} %get-tuple-element.6.phi_ref, f32[72,12,2,128]{3,2,1,0:T(2,128)} %get-tuple-element.7.force_ref), custom_call_target="tpu_custom_call" | custom-call | tf_op jit(solution)/shard_map/write_out/pallas_call | solution.py:425
where the time goes:
time: 17.6 us; the launch traced here: 17.4 us
  Pallas kernels  16.8 us (95%)
  between operations  0.64 us (4%)
    pallas_call x1, Pallas kernels, body(): pl.pallas_call(lambda *refs: kernel(nt, nz, *refs), name='wilson', out_sh...  14.5 us
    pallas_call x1, Pallas kernels, body(): pl.pallas_call(write_out, name='write_out', out_shape=(jax.ShapeDtypeStru...  2.27 us

commit v1 on v0

--- a/solution.py
+++ b/solution.py
@@ -404,10 +404,10 @@
         lambda *refs: kernel(nt, nz, *refs),
         name="wilson",
         out_shape=(
-            jax.ShapeDtypeStruct((24, parts, nz, LANES), jnp.float32),
-            jax.ShapeDtypeStruct((u.shape[0], parts, nz, LANES), jnp.float32),
+            pltpu.VMEM((24, parts, nz, LANES), jnp.float32),
+            pltpu.VMEM((u.shape[0], parts, nz, LANES), jnp.float32),
         ),
-        in_specs=[pl.BlockSpec(memory_space=pl.ANY)] * 3,
+        in_specs=[pl.BlockSpec(memory_space=pltpu.HBM)] * 3,
         out_specs=(pl.BlockSpec(memory_space=pltpu.VMEM),) * 2,
         scratch_shapes=[
             held(x), held(u), held(c),
@@ -420,7 +420,7 @@
             pltpu.SemaphoreType.DMA((6,)),
             pltpu.SemaphoreType.DMA((6,)),
         ],
-        compiler_params=pltpu.CompilerParams(collective_id=0, has_side_effects=True),
+        compiler_params=pltpu.CompilerParams(collective_id=0, has_side_effects=True, vmem_limit_bytes=56 * 1024 * 1024),
     )(x, u, c)
     applied, force = pl.pallas_call(
         write_out,
@@ -432,6 +432,7 @@
         in_specs=[pl.BlockSpec(memory_space=pltpu.VMEM)] * 2,
         out_specs=(pl.BlockSpec(memory_space=pl.ANY),) * 2,
         scratch_shapes=[pltpu.SemaphoreType.DMA((2,))],
+        compiler_params=pltpu.CompilerParams(vmem_limit_bytes=8 * 1024 * 1024),
     )(phi, anti)
     return applied.reshape(spinor.shape), force.reshape(links.shape)
 

time: 17.6 us -> 15.3 us (0.87)
  Pallas kernels: 16.8 us -> 14.5 us
    pallas_call x1, Pallas kernels: 2.27 us -> 1.01 us  [body(): pl.pallas_call(write_out, name='write_out', out_shape=(jax.ShapeDtypeStru...]
    pallas_call x1, Pallas kernels: 14.5 us -> 13.5 us  [body(): pl.pallas_call(lambda *refs: kernel(nt, nz, *refs), name='wilson', out_sh...]
where the time goes in v1:
time: 15.3 us; the launch traced here: 15.2 us
  Pallas kernels  14.5 us (95%)
  between operations  0.64 us (4%)
    pallas_call x1, Pallas kernels, body(): pl.pallas_call(lambda *refs: kernel(nt, nz, *refs), name='wilson', out_sh...  13.5 us
    pallas_call x1, Pallas kernels, body(): pl.pallas_call(write_out, name='write_out', out_shape=(jax.ShapeDtypeStru...  1.01 us

profile of v1, /device:TPU:1, one launch (start us, length us, event | category | flops | bytes accessed | tf_op | source)
XLA Modules:
  0.0 15.2 jit_solution(7498957592651079974)
XLA Ops:
  0.6 13.5 %wilson.1 = (f32[24,12,2,128]{3,2,1,0:T(2,128)S(1)}, f32[72,12,2,128]{3,2,1,0:T(2,128)S(1)}) custom-call(f32[24,2,2,768]{3,2,1,0:T(2,128)} %bitcast.7, f32[72,2,2,768]{3,2,1,0:T(2,128)} %bitcast.6, f32[144,2,2,768]{3,2,1,0:T(2,128)} %bitcast.5), custom_call_target="tpu_custom_call" | custom-call | tf_op jit(solution)/shard_map/wilson/pallas_call | solution.py:403
  14.2 1.0 %write_out.1 = (f32[24,2,2,768]{3,2,1,0:T(2,128)}, f32[72,2,2,768]{3,2,1,0:T(2,128)}) custom-call(f32[24,12,2,128]{3,2,1,0:T(2,128)S(1)} %get-tuple-element.6.phi_ref, f32[72,12,2,128]{3,2,1,0:T(2,128)S(1)} %get-tuple-element.7.force_ref), custom_call_target="tpu_custom_call" | custom-call | tf_op jit(solution)/shard_map/write_out/pallas_call | solution.py:425

commit v2 on v1

--- a/solution.py
+++ b/solution.py
@@ -99,31 +99,35 @@
 
 
 def kernel(nt, nz, x_hbm, u_hbm, c_hbm, phi_out, force_out, psi_in, link_in, clov_in, hm, hp, bl,
-           sh_hm, sh_bl, prod, acc, hphi, sh_hphi, face_out, face_in, in_sem, send_sem, recv_sem):
+           sh_hm, sh_bl, prod, acc, hphi, sh_hphi, face_out, face_in, in_sem, send_sem, recv_sem, ready):
     psi, link, clov, out_ref, force_ref = map(flat, (psi_in, link_in, clov_in, phi_out, force_out))
     rows = psi.shape[1]
     face_t = rows // nt
     face_z = rows // nz
+    line = face_t // nz
     chunks = rows // TILE
     t_place, z_place = lax.axis_index("ta"), lax.axis_index("gz")
     t_count, z_count = lax.axis_size("ta"), lax.axis_size("gz")
-    t_next = (lax.rem(t_place + 1, t_count), z_place)
-    t_prev = (lax.rem(t_place + t_count - 1, t_count), z_place)
-    z_next = (t_place, lax.rem(z_place + 1, z_count))
-    z_prev = (t_place, lax.rem(z_place + z_count - 1, z_count))
     low_sign = jnp.where(t_place == 0, -1.0, 1.0).astype(jnp.float32)
     high_sign = jnp.where(t_place == t_count - 1, -1.0, 1.0).astype(jnp.float32)
 
+    near = (
+        (lax.rem(t_place + t_count - 1, t_count), z_place),
+        (lax.rem(t_place + 1, t_count), z_place),
+        (t_place, lax.rem(z_place + z_count - 1, z_count)),
+        (t_place, lax.rem(z_place + 1, z_count)),
+    )
+    T_PREV, T_NEXT, Z_PREV, Z_NEXT = range(4)
+    first = (t_place > 0, t_place == t_count - 1, z_place > 0, z_place == z_count - 1)
     barrier = pltpu.get_barrier_semaphore()
-    for target in (t_next, t_prev, z_next, z_prev):
-        pl.semaphore_signal(barrier, inc=1, device_id=target, device_id_type=MESH)
 
     groups = [(x_hbm, psi_in)]
     for mu in range(4):
         part = pl.ds(18 * mu, 18)
         groups.append((u_hbm.at[part], link_in.at[part]))
     groups.append((c_hbm, clov_in))
-    for n in (0, 3, 4, 1, 2, 5):
+
+    def fetch(n):
         for src, dst in parts_of(*groups[n]):
             pltpu.make_async_copy(src, dst, in_sem.at[n]).start()
 
@@ -131,11 +135,37 @@
         held = groups[n][1]
         pltpu.make_async_copy(held, held, in_sem.at[n]).wait()
 
+    for k in range(4):
+        @pl.when(jnp.logical_not(first[k]))
+        def _():
+            pl.semaphore_signal(barrier, inc=1, device_id=near[k], device_id_type=MESH)
+
+    for n in (0, 3, 4):
+        fetch(n)
+    greeters = sum(f.astype(jnp.int32) for f in first)
+
+    @pl.when(greeters > 0)
+    def _():
+        pl.semaphore_wait(barrier, greeters)
+
+    for k in range(4):
+        @pl.when(first[k])
+        def _():
+            pl.semaphore_signal(ready.at[k ^ 1], inc=1, device_id=near[k], device_id_type=MESH)
+    for n in (1, 2, 5):
+        fetch(n)
+
     def window(v):
         return pl.ds(pl.multiple_of(v * TILE, TILE), TILE)
 
     def load_spinor(ref, at):
         return [[(ref[3 * s + c, at, :], ref[12 + 3 * s + c, at, :]) for c in range(3)] for s in range(4)]
+
+    def store_spinor(ref, at, value):
+        for s in range(4):
+            for c in range(3):
+                ref[3 * s + c, at, :] = value[s][c][0]
+                ref[12 + 3 * s + c, at, :] = value[s][c][1]
 
     def load_half(ref, mu, at):
         return [[(ref[mu, 3 * s + c, at, :], ref[mu, 6 + 3 * s + c, at, :]) for c in range(3)] for s in range(2)]
@@ -188,21 +218,77 @@
     def t_behind(src, dst, c):
         dst[3, c, pl.ds(face_t, rows - face_t), :] = src[3, c, pl.ds(0, rows - face_t), :]
 
-    def for_each(count, body):
+    def for_each(count, body, low=0):
         def step(i, carry):
             body(i)
             return carry
 
-        lax.fori_loop(0, count, step, 0)
-
-    targets = (t_prev, t_next, z_prev, z_next, t_prev, z_prev)
-    sends = [
-        pltpu.make_async_remote_copy(
-            src_ref=face_out.at[k], dst_ref=face_in.at[k], send_sem=send_sem.at[k],
-            recv_sem=recv_sem.at[k], device_id=targets[k], device_id_type=MESH,
+        lax.fori_loop(low, count, step, 0)
+
+    t_last, z_last = nt - 1, nz - 1
+    messages = {
+        "a0": (T_PREV, [(0, 0)], [(t_last, 0)]),
+        "a1": (T_PREV, [(0, z) for z in range(1, nz)], [(t_last, z) for z in range(1, nz)]),
+        "b0": (T_NEXT, [(t_last, 0)], [(0, 0)]),
+        "b1": (T_NEXT, [(t_last, z) for z in range(1, nz)], [(0, z) for z in range(1, nz)]),
+        "c0": (Z_PREV, [(0, 0)], [(0, z_last)]),
+        "c1": (Z_PREV, [(t, 0) for t in range(1, nt)], [(t, z_last) for t in range(1, nt)]),
+        "d0": (Z_NEXT, [(0, z_last)], [(0, 0)]),
+        "d1": (Z_NEXT, [(t, z_last) for t in range(1, nt)], [(t, 0) for t in range(1, nt)]),
+        "e0": (Z_PREV, [(t, 0) for t in range(t_last)], [(t, z_last) for t in range(t_last)]),
+        "e1": (Z_PREV, [(t_last, 0)], [(t_last, z_last)]),
+        "f0": (T_PREV, [(0, z) for z in range(z_last)], [(t_last, z) for z in range(z_last)]),
+        "f1": (T_PREV, [(0, z_last)], [(t_last, z_last)]),
+    }
+    names = list(messages)
+
+    def place(name, i, c):
+        return names.index(name), pl.ds((12 * i + c) * line, line)
+
+    def lines(at):
+        return pl.ds(at[0] * face_t + at[1], line, nz)
+
+    def pack(name, src, mu):
+        for i, at in enumerate(messages[name][1]):
+            for c in range(12):
+                k, held = place(name, i, c)
+                face_out[k, held, :] = src[mu, c, lines(at), :]
+
+    def unpack(name, dst, mu, change=lambda value, at, c: value):
+        for i, at in enumerate(messages[name][2]):
+            for c in range(12):
+                k, held = place(name, i, c)
+                dst[mu, c, lines(at), :] = change(face_in[k, held, :], at, c)
+
+    def copy_of(name):
+        k, size = names.index(name), 12 * line * len(messages[name][1])
+        return pltpu.make_async_remote_copy(
+            src_ref=face_out.at[k, pl.ds(0, size)], dst_ref=face_in.at[k, pl.ds(0, size)], send_sem=send_sem.at[k],
+            recv_sem=recv_sem.at[k], device_id=near[messages[name][0]], device_id_type=MESH,
         )
-        for k in range(6)
-    ]
+
+    copies = {name: copy_of(name) for name in names}
+    greeted = set()
+
+    def send_early(*some):
+        for name in some:
+            pl.when(first[messages[name][0]])(copies[name].start)
+
+    def send_late(*some):
+        for name in some:
+            side = messages[name][0]
+
+            @pl.when(jnp.logical_not(first[side]))
+            def _():
+                if side not in greeted:
+                    pl.semaphore_wait(ready.at[side], 1)
+                copies[name].start()
+
+            greeted.add(side)
+
+    def received(*some):
+        for name in some:
+            copies[name].wait_recv()
 
     def project(mu, v):
         at = window(v)
@@ -212,37 +298,31 @@
         store_half(hp, mu, at, ahead)
         store_half(bl, mu, at, mat_vec(load_link(mu, at), ahead, True))
 
-    def face(k, c, size):
-        return k, pl.ds(c * size, size)
-
     arrived(0)
     arrived(3)
     for_each(chunks, lambda v: project(2, v))
-    for c in range(12):
-        k, at = face(3, c, face_z)
-        face_out[k, at, :] = bl[2, c, pl.ds(nz - 1, face_z, nz), :]
-    pl.semaphore_wait(barrier, 4)
-    sends[3].start()
-    for c in range(12):
-        k, at = face(2, c, face_z)
-        face_out[k, at, :] = hm[2, c, pl.ds(0, face_z, nz), :]
+    for name in ("d0", "d1"):
+        pack(name, bl, 2)
+    for name in ("c0", "c1"):
+        pack(name, hm, 2)
+    send_early("d0")
     arrived(4)
     for_each(chunks, lambda v: project(3, v))
-    for c in range(12):
-        k, at = face(0, c, face_t)
-        face_out[k, at, :] = hm[3, c, 0:face_t, :]
-        k, at = face(1, c, face_t)
-        face_out[k, at, :] = bl[3, c, rows - face_t:rows, :]
-    sends[1].start()
-    sends[0].start()
-    sends[2].start()
+    for name in ("a0", "a1"):
+        pack(name, hm, 3)
+    for name in ("b0", "b1"):
+        pack(name, bl, 3)
+    send_early("b0", "a0", "c0")
+    send_late("b0", "d0")
+    send_early("d1", "b1", "a1", "c1")
+    send_late("b1", "d1")
 
     arrived(1)
     for_each(chunks, lambda v: project(0, v))
     arrived(2)
     for_each(chunks, lambda v: project(1, v))
 
-    def shifts(c):
+    for c in range(12):
         sh_hm[0, c] = shift_x1(hm[0, c], 1)
         sh_bl[0, c] = shift_x1(bl[0, c], -1)
         sh_hm[1, c] = shift_x2(hm[1, c], 1)
@@ -252,8 +332,6 @@
         t_ahead(hm, sh_hm, c)
         t_behind(bl, sh_bl, c)
 
-    for_each(12, shifts)
-
     def hop(mu, at, total):
         ahead = mat_vec(load_link(mu, at), load_half(sh_hm, mu, at), False)
         store_half(prod, mu, at, ahead)
@@ -262,12 +340,15 @@
 
     zero = jnp.zeros((TILE, LANES), jnp.float32)
 
+    def nothing():
+        return [[(zero, zero)] * 3 for _ in range(4)]
+
     arrived(5)
 
     def local(v):
         at = window(v)
         field = load_spinor(psi, at)
-        total = [[(zero, zero)] * 3 for _ in range(4)]
+        total = nothing()
         for mu in (0, 1):
             total = hop(mu, at, total)
         for s in range(4):
@@ -286,60 +367,75 @@
 
     for_each(chunks, local)
 
-    for k in (0, 1, 3):
-        sends[k].wait_recv()
-    for c in range(12):
-        k, at = face(0, c, face_t)
-        sh_hm[3, c, pl.ds(rows - face_t, face_t), :] = face_in[k, at, :] * high_sign
-        k, at = face(1, c, face_t)
-        sh_bl[3, c, pl.ds(0, face_t), :] = face_in[k, at, :] * low_sign
-        k, at = face(3, c, face_z)
-        sh_bl[2, c, pl.ds(0, face_z, nz), :] = face_in[k, at, :]
-        sh_hm[2, c, pl.ds(nz - 1, face_z, nz), :] = jnp.zeros((face_z, LANES), jnp.float32)
-
-    def finish(v, early):
-        at = window(v)
-        total = [[(zero, zero)] * 3 for _ in range(4)]
-        for mu in (2, 3):
-            total = hop(mu, at, total)
+    def with_hops(mu, at):
+        total = hop(mu, at, nothing())
         held = load_spinor(acc, at)
-        phi = [
+        return [
             [(held[s][c][0] - 0.5 * total[s][c][0], held[s][c][1] - 0.5 * total[s][c][1]) for c in range(3)]
             for s in range(4)
         ]
-        if early:
-            store_half(hphi, 2, at, half(2, phi, 1.0))
-            return
-        for s in range(4):
-            for c in range(3):
-                out_ref[3 * s + c, at, :] = phi[s][c][0]
-                out_ref[12 + 3 * s + c, at, :] = phi[s][c][1]
+
+    def partial(across, along, v):
+        at = window(v)
+        store_half(hphi, along, at, half(along, with_hops(across, at), 1.0))
+
+    def signed(sign):
+        return lambda value, at, c: value * sign
+
+    low_chunks = -(-face_t // TILE)
+    high_chunk = (rows - face_t) // TILE
+
+    send_late("a0", "c0", "a1", "c1")
+
+    received("a0")
+    unpack("a0", sh_hm, 3, signed(high_sign))
+    for_each(chunks, lambda v: partial(3, 2, v), high_chunk)
+    pack("e1", hphi, 2)
+    copies["e1"].start()
+    received("b0")
+    unpack("b0", sh_bl, 3, signed(low_sign))
+    for_each(-(-(rows - face_t) // TILE), lambda v: partial(3, 2, v))
+    pack("e0", hphi, 2)
+    copies["e0"].start()
+
+    received("c0")
+    unpack("c0", sh_hm, 2)
+    for_each(low_chunks, lambda v: partial(2, 3, v))
+    pack("f1", hphi, 3)
+    copies["f1"].start()
+    received("d0")
+    unpack("d0", sh_bl, 2)
+    for_each(low_chunks, lambda v: partial(2, 3, v))
+    pack("f0", hphi, 3)
+    copies["f0"].start()
+
+    received("a1", "b1")
+    unpack("a1", sh_hm, 3, signed(high_sign))
+    unpack("b1", sh_bl, 3, signed(low_sign))
+
+    def gather(v):
+        at = window(v)
+        store_spinor(acc, at, with_hops(3, at))
+
+    for_each(chunks, gather)
+    received("c1", "d1")
+    unpack("c1", sh_hm, 2)
+    unpack("d1", sh_bl, 2)
+
+    def finish(v):
+        at = window(v)
+        phi = with_hops(2, at)
+        store_spinor(out_ref, at, phi)
         for mu in range(4):
             store_half(hphi, mu, at, half(mu, phi, 1.0))
 
-    for_each(chunks, lambda v: finish(v, True))
+    for_each(chunks, finish)
+
     for c in range(12):
-        k, at = face(5, c, face_z)
-        face_out[k, at, :] = hphi[2, c, pl.ds(0, face_z, nz), :]
-    sends[5].start()
-
-    sends[2].wait_recv()
-    for c in range(12):
-        k, at = face(2, c, face_z)
-        sh_hm[2, c, pl.ds(nz - 1, face_z, nz), :] = face_in[k, at, :]
-    for_each(chunks, lambda v: finish(v, False))
-    for c in range(12):
-        k, at = face(4, c, face_t)
-        face_out[k, at, :] = hphi[3, c, 0:face_t, :]
-    sends[4].start()
-
-    def shifts_phi(c):
         sh_hphi[0, c] = shift_x1(hphi[0, c], 1)
         sh_hphi[1, c] = shift_x2(hphi[1, c], 1)
         z_ahead(hphi, sh_hphi, c)
         t_ahead(hphi, sh_hphi, c)
-
-    for_each(12, shifts_phi)
 
     def force(mu, v):
         at = window(v)
@@ -372,18 +468,16 @@
     for mu in (0, 1):
         for_each(chunks, lambda v: force(mu, v))
 
-    sends[4].wait_recv()
-    for c in range(12):
-        k, at = face(4, c, face_t)
-        sh_hphi[3, c, pl.ds(rows - face_t, face_t), :] = face_in[k, at, :] * high_sign
+    for name in ("f0", "f1"):
+        received(name)
+        unpack(name, sh_hphi, 3, lambda value, at, c: value * high_sign - bl[3, c, lines(at), :])
     for_each(chunks, lambda v: force(3, v))
-    sends[5].wait_recv()
-    for c in range(12):
-        k, at = face(5, c, face_z)
-        sh_hphi[2, c, pl.ds(nz - 1, face_z, nz), :] = face_in[k, at, :]
+    for name in ("e0", "e1"):
+        received(name)
+        unpack(name, sh_hphi, 2, lambda value, at, c: value - bl[2, c, lines(at), :])
     for_each(chunks, lambda v: force(2, v))
-    for k in range(6):
-        sends[k].wait_send()
+    for name in names:
+        copies[name].wait_send()
 
 
 def body(spinor, links, clover):
@@ -392,7 +486,8 @@
     x, u, c = (a.reshape((-1,) + sites) for a in (spinor, links, clover))
     parts = nt * (sites[2] // LANES)
     rows = parts * nz
-    face = max(rows // nt, rows // nz)
+    assert nt > 1 and nz > 1
+    face = max(nt - 1, nz - 1) * rows // (nt * nz)
 
     def halves():
         return pltpu.VMEM((4, 12, rows, LANES), jnp.float32)
@@ -414,11 +509,12 @@
             halves(), halves(), halves(), halves(), halves(), halves(),
             pltpu.VMEM((24, rows, LANES), jnp.float32),
             halves(), halves(),
-            pltpu.VMEM((6, 12 * face, LANES), jnp.float32),
-            pltpu.VMEM((6, 12 * face, LANES), jnp.float32),
+            pltpu.VMEM((12, 12 * face, LANES), jnp.float32),
+            pltpu.VMEM((12, 12 * face, LANES), jnp.float32),
             pltpu.SemaphoreType.DMA((6,)),
-            pltpu.SemaphoreType.DMA((6,)),
-            pltpu.SemaphoreType.DMA((6,)),
+            pltpu.SemaphoreType.DMA((12,)),
+            pltpu.SemaphoreType.DMA((12,)),
+            pltpu.SemaphoreType.REGULAR((4,)),
         ],
         compiler_params=pltpu.CompilerParams(collective_id=0, has_side_effects=True, vmem_limit_bytes=56 * 1024 * 1024),
     )(x, u, c)

time: 15.3 us -> 13.5 us (0.88)
  Pallas kernels: 14.5 us -> 12.7 us
    pallas_call x1, Pallas kernels: 13.5 us -> 11.7 us  [body(): pl.pallas_call(lambda *refs: kernel(nt, nz, *refs), name='wilson', out_sh...]
where the time goes in v2:
time: 13.5 us; the launch traced here: 13.4 us
  Pallas kernels  12.7 us (94%)
  between operations  0.64 us (5%)
    pallas_call x1, Pallas kernels, body(): pl.pallas_call(lambda *refs: kernel(nt, nz, *refs), name='wilson', out_sh...  11.7 us
    pallas_call x1, Pallas kernels, body(): pl.pallas_call(write_out, name='write_out', out_shape=(jax.ShapeDtypeStru...  1.01 us

profile of v2, /device:TPU:1, one launch (start us, length us, event | category | flops | bytes accessed | tf_op | source)
XLA Modules:
  0.0 13.4 jit_solution(6217430030306540581)
XLA Ops:
  0.6 11.7 %wilson.1 = (f32[24,12,2,128]{3,2,1,0:T(2,128)S(1)}, f32[72,12,2,128]{3,2,1,0:T(2,128)S(1)}) custom-call(f32[24,2,2,768]{3,2,1,0:T(2,128)} %bitcast.7, f32[72,2,2,768]{3,2,1,0:T(2,128)} %bitcast.6, f32[144,2,2,768]{3,2,1,0:T(2,128)} %bitcast.5), custom_call_target="tpu_custom_call" | custom-call | tf_op jit(solution)/shard_map/wilson/pallas_call | solution.py:498
  12.4 1.0 %write_out.1 = (f32[24,2,2,768]{3,2,1,0:T(2,128)}, f32[72,2,2,768]{3,2,1,0:T(2,128)}) custom-call(f32[24,12,2,128]{3,2,1,0:T(2,128)S(1)} %get-tuple-element.6.phi_ref, f32[72,12,2,128]{3,2,1,0:T(2,128)S(1)} %get-tuple-element.7.force_ref), custom_call_target="tpu_custom_call" | custom-call | tf_op jit(solution)/shard_map/write_out/pallas_call | solution.py:521

commit v3 on v2

--- a/solution.py
+++ b/solution.py
@@ -99,7 +99,8 @@
 
 
 def kernel(nt, nz, x_hbm, u_hbm, c_hbm, phi_out, force_out, psi_in, link_in, clov_in, hm, hp, bl,
-           sh_hm, sh_bl, prod, acc, hphi, sh_hphi, face_out, face_in, in_sem, send_sem, recv_sem, ready):
+           sh_hm, sh_bl, prod, acc, hphi, sh_hphi, face_out, face_in, link_out, corner_in, in_sem,
+           send_sem, recv_sem, ready):
     psi, link, clov, out_ref, force_ref = map(flat, (psi_in, link_in, clov_in, phi_out, force_out))
     rows = psi.shape[1]
     face_t = rows // nt
@@ -111,13 +112,13 @@
     low_sign = jnp.where(t_place == 0, -1.0, 1.0).astype(jnp.float32)
     high_sign = jnp.where(t_place == t_count - 1, -1.0, 1.0).astype(jnp.float32)
 
+    T_PREV, T_NEXT, Z_PREV, Z_NEXT = range(4)
     near = (
         (lax.rem(t_place + t_count - 1, t_count), z_place),
         (lax.rem(t_place + 1, t_count), z_place),
         (t_place, lax.rem(z_place + z_count - 1, z_count)),
         (t_place, lax.rem(z_place + 1, z_count)),
     )
-    T_PREV, T_NEXT, Z_PREV, Z_NEXT = range(4)
     first = (t_place > 0, t_place == t_count - 1, z_place > 0, z_place == z_count - 1)
     barrier = pltpu.get_barrier_semaphore()
 
@@ -135,10 +136,19 @@
         held = groups[n][1]
         pltpu.make_async_copy(held, held, in_sem.at[n]).wait()
 
-    for k in range(4):
-        @pl.when(jnp.logical_not(first[k]))
+    even = lax.rem(t_place, 2) == 0
+    relay = jnp.logical_and(even, t_place > 0)
+    t_after = near[T_NEXT][0]
+    relayed = jnp.logical_and(lax.rem(t_after, 2) == 0, t_after > 0)
+    z_low, z_high = z_place == 0, z_place == z_count - 1
+
+    def greet(k, when):
+        @pl.when(jnp.logical_and(when, jnp.logical_not(first[k])))
         def _():
             pl.semaphore_signal(barrier, inc=1, device_id=near[k], device_id_type=MESH)
+
+    for k in range(4):
+        greet(k, jnp.logical_not(relay) if k == Z_PREV else True)
 
     for n in (0, 3, 4):
         fetch(n)
@@ -148,6 +158,7 @@
     def _():
         pl.semaphore_wait(barrier, greeters)
 
+    greet(Z_PREV, relay)
     for k in range(4):
         @pl.when(first[k])
         def _():
@@ -268,23 +279,45 @@
         )
 
     copies = {name: copy_of(name) for name in names}
-    greeted = set()
-
-    def send_early(*some):
-        for name in some:
-            pl.when(first[messages[name][0]])(copies[name].start)
-
-    def send_late(*some):
-        for name in some:
-            side = messages[name][0]
-
-            @pl.when(jnp.logical_not(first[side]))
-            def _():
-                if side not in greeted:
-                    pl.semaphore_wait(ready.at[side], 1)
-                copies[name].start()
-
-            greeted.add(side)
+
+    def corner_of(k, held, target):
+        size = pl.ds(0, held.shape[0])
+        return pltpu.make_async_remote_copy(
+            src_ref=held, dst_ref=corner_in.at[k, size], send_sem=send_sem.at[len(names) + k],
+            recv_sem=recv_sem.at[len(names) + k], device_id=target, device_id_type=MESH,
+        )
+
+    t_before = near[T_PREV][0]
+    corners = [
+        corner_of(0, face_out.at[names.index("d0"), pl.ds(0, 12 * line)], (t_before, near[Z_NEXT][1])),
+        corner_of(1, face_out.at[names.index("c0"), pl.ds(0, 12 * line)], (t_before, near[Z_PREV][1])),
+        corner_of(2, link_out, near[T_PREV]),
+    ]
+    relay_high, relay_low = jnp.logical_and(relay, z_high), jnp.logical_and(relay, z_low)
+    relayed_high, relayed_low = jnp.logical_and(relayed, z_high), jnp.logical_and(relayed, z_low)
+    def sender(mine):
+        greeted = set()
+
+        def early(*some):
+            for name in some:
+                pl.when(jnp.logical_and(mine, first[messages[name][0]]))(copies[name].start)
+
+        def late(*some):
+            for name in some:
+                side = messages[name][0]
+
+                @pl.when(jnp.logical_and(mine, jnp.logical_not(first[side])))
+                def _():
+                    if side not in greeted:
+                        pl.semaphore_wait(ready.at[side], 1)
+                    copies[name].start()
+
+                greeted.add(side)
+
+        return early, late
+
+    even_early, even_late = sender(even)
+    odd_early, odd_late = sender(jnp.logical_not(even))
 
     def received(*some):
         for name in some:
@@ -298,24 +331,41 @@
         store_half(hp, mu, at, ahead)
         store_half(bl, mu, at, mat_vec(load_link(mu, at), ahead, True))
 
+    def behind(v):
+        at = window(v)
+        store_half(hm, 2, at, half(2, load_spinor(psi, at), -1.0))
+
+    inner = jnp.logical_not(first[Z_NEXT])
     arrived(0)
+    for_each(chunks, behind)
+    for name in ("c0", "c1"):
+        pack(name, hm, 2)
+    for name in ("c0", "c1"):
+        pl.when(jnp.logical_and(inner, first[Z_PREV]))(copies[name].start)
     arrived(3)
     for_each(chunks, lambda v: project(2, v))
     for name in ("d0", "d1"):
         pack(name, bl, 2)
-    for name in ("c0", "c1"):
-        pack(name, hm, 2)
-    send_early("d0")
+    pl.when(relay_high)(corners[0].start)
+    even_early("d0")
+    for name in ("c0", "d1"):
+        pl.when(relay_high)(copies[name].start)
+    for name in ("d1", "c0"):
+        pl.when(jnp.logical_and(z_high, t_place == 0))(copies[name].start)
     arrived(4)
     for_each(chunks, lambda v: project(3, v))
     for name in ("a0", "a1"):
         pack(name, hm, 3)
     for name in ("b0", "b1"):
         pack(name, bl, 3)
-    send_early("b0", "a0", "c0")
-    send_late("b0", "d0")
-    send_early("d1", "b1", "a1", "c1")
-    send_late("b1", "d1")
+    even_early("b0", "a0", "a1", "b1")
+    even_late("b0", "b1")
+    odd_early("a0", "b0", "a1", "b1", "d0")
+    for c in range(18):
+        link_out[c * line:(c + 1) * line, :] = link[36 + c, lines((0, z_last)), :]
+    pl.when(relay_high)(corners[2].start)
+    pl.when(jnp.logical_and(even, z_high))(copies["c1"].start)
+    pl.when(jnp.logical_and(jnp.logical_not(even), z_high))(copies["c0"].start)
 
     arrived(1)
     for_each(chunks, lambda v: project(0, v))
@@ -343,6 +393,8 @@
     def nothing():
         return [[(zero, zero)] * 3 for _ in range(4)]
 
+    even_late("d0", "d1")
+    odd_late("d0", "d1")
     arrived(5)
 
     def local(v):
@@ -385,7 +437,32 @@
     low_chunks = -(-face_t // TILE)
     high_chunk = (rows - face_t) // TILE
 
-    send_late("a0", "c0", "a1", "c1")
+    odd_early("d1")
+    pl.when(jnp.logical_and(jnp.logical_not(even), z_high))(copies["c1"].start)
+    odd_late("b0", "b1")
+    for c in range(12):
+        sh_bl[2, c, lines((0, 0)), :] = jnp.zeros((line, LANES), jnp.float32)
+        sh_hm[2, c, lines((0, z_last)), :] = jnp.zeros((line, LANES), jnp.float32)
+
+    def send_f(name, when):
+        @pl.when(when)
+        def _():
+            for_each(low_chunks, lambda v: partial(2, 3, v))
+            pack(name, hphi, 3)
+            copies[name].start()
+
+    send_f("f0", relay_low)
+    send_f("f1", relay_high)
+
+    @pl.when(jnp.logical_and(z_low, True))
+    def _():
+        pl.semaphore_wait(ready.at[Z_PREV], 1)
+        pl.when(relay)(corners[1].start)
+        copies["c0"].start()
+        copies["c1"].start()
+
+    even_late("a0", "a1")
+    odd_late("a0", "a1")
 
     received("a0")
     unpack("a0", sh_hm, 3, signed(high_sign))
@@ -398,16 +475,19 @@
     pack("e0", hphi, 2)
     copies["e0"].start()
 
-    received("c0")
-    unpack("c0", sh_hm, 2)
-    for_each(low_chunks, lambda v: partial(2, 3, v))
-    pack("f1", hphi, 3)
-    copies["f1"].start()
-    received("d0")
-    unpack("d0", sh_bl, 2)
-    for_each(low_chunks, lambda v: partial(2, 3, v))
-    pack("f0", hphi, 3)
-    copies["f0"].start()
+    def take_c():
+        received("c0")
+        unpack("c0", sh_hm, 2)
+        send_f("f1", jnp.logical_not(relay_high))
+
+    def take_d():
+        received("d0")
+        unpack("d0", sh_bl, 2)
+        send_f("f0", jnp.logical_not(relay_low))
+
+    pl.when(jnp.logical_not(z_low))(take_d)
+    take_c()
+    pl.when(z_low)(take_d)
 
     received("a1", "b1")
     unpack("a1", sh_hm, 3, signed(high_sign))
@@ -471,6 +551,35 @@
     for name in ("f0", "f1"):
         received(name)
         unpack(name, sh_hphi, 3, lambda value, at, c: value * high_sign - bl[3, c, lines(at), :])
+
+    def corner(k, c):
+        return corner_in[k, c * line:(c + 1) * line, :]
+
+    def corner_half(k):
+        return [[(corner(k, 3 * s + c), corner(k, 6 + 3 * s + c)) for c in range(3)] for s in range(2)]
+
+    none = [[(0.0, 0.0)] * 3 for _ in range(4)]
+
+    def add_corner(value, sign, z):
+        extra = half(3, add_whole(2, none, value, sign), 1.0)
+        for s in range(2):
+            for c in range(3):
+                for n, part in enumerate(extra[s][c]):
+                    place = 3, 6 * n + 3 * s + c, lines((t_last, z)), slice(None)
+                    sh_hphi[place] = sh_hphi[place] - 0.5 * high_sign * part
+
+    @pl.when(relayed_low)
+    def _():
+        corners[0].wait_recv()
+        add_corner(corner_half(0), 1.0, 0)
+
+    @pl.when(relayed_high)
+    def _():
+        corners[2].wait_recv()
+        corners[1].wait_recv()
+        near_link = [[(corner(2, 3 * a + b), corner(2, 9 + 3 * a + b)) for b in range(3)] for a in range(3)]
+        add_corner(mat_vec(near_link, corner_half(1), False), -1.0, z_last)
+
     for_each(chunks, lambda v: force(3, v))
     for name in ("e0", "e1"):
         received(name)
@@ -478,6 +587,8 @@
     for_each(chunks, lambda v: force(2, v))
     for name in names:
         copies[name].wait_send()
+    for k, mine in enumerate((relay_high, relay_low, relay_high)):
+        pl.when(mine)(corners[k].wait_send)
 
 
 def body(spinor, links, clover):
@@ -487,7 +598,8 @@
     parts = nt * (sites[2] // LANES)
     rows = parts * nz
     assert nt > 1 and nz > 1
-    face = max(nt - 1, nz - 1) * rows // (nt * nz)
+    line = rows // (nt * nz)
+    face = max(nt - 1, nz - 1) * line
 
     def halves():
         return pltpu.VMEM((4, 12, rows, LANES), jnp.float32)
@@ -511,9 +623,11 @@
             halves(), halves(),
             pltpu.VMEM((12, 12 * face, LANES), jnp.float32),
             pltpu.VMEM((12, 12 * face, LANES), jnp.float32),
+            pltpu.VMEM((18 * line, LANES), jnp.float32),
+            pltpu.VMEM((3, 18 * line, LANES), jnp.float32),
             pltpu.SemaphoreType.DMA((6,)),
-            pltpu.SemaphoreType.DMA((12,)),
-            pltpu.SemaphoreType.DMA((12,)),
+            pltpu.SemaphoreType.DMA((15,)),
+            pltpu.SemaphoreType.DMA((15,)),
             pltpu.SemaphoreType.REGULAR((4,)),
         ],
         compiler_params=pltpu.CompilerParams(collective_id=0, has_side_effects=True, vmem_limit_bytes=56 * 1024 * 1024),

time: 13.5 us -> 12.7 us (0.941)
  the two profiles are of different devices: /device:TPU:1 before, /device:TPU:0 now
where the time goes in v3:
time: 12.7 us; the launch traced here: 12.5 us
  Pallas kernels  11.9 us (94%)
  between operations  0.64 us (5%)
    pallas_call x1, Pallas kernels, body(): pl.pallas_call(lambda *refs: kernel(nt, nz, *refs), name='wilson', out_sh...  10.9 us
    pallas_call x1, Pallas kernels, body(): pl.pallas_call(write_out, name='write_out', out_shape=(jax.ShapeDtypeStru...  1.01 us

profile of v3, /device:TPU:0, one launch (start us, length us, event | category | flops | bytes accessed | tf_op | source)
XLA Modules:
  0.0 12.5 jit_solution(11095994603412519439)
XLA Ops:
  0.6 10.9 %wilson.1 = (f32[24,12,2,128]{3,2,1,0:T(2,128)S(1)}, f32[72,12,2,128]{3,2,1,0:T(2,128)S(1)}) custom-call(f32[24,2,2,768]{3,2,1,0:T(2,128)} %bitcast.7, f32[72,2,2,768]{3,2,1,0:T(2,128)} %bitcast.6, f32[144,2,2,768]{3,2,1,0:T(2,128)} %bitcast.5), custom_call_target="tpu_custom_call" | custom-call | tf_op jit(solution)/shard_map/wilson/pallas_call | solution.py:610
  11.5 1.0 %write_out.1 = (f32[24,2,2,768]{3,2,1,0:T(2,128)}, f32[72,2,2,768]{3,2,1,0:T(2,128)}) custom-call(f32[24,12,2,128]{3,2,1,0:T(2,128)S(1)} %get-tuple-element.6.phi_ref, f32[72,12,2,128]{3,2,1,0:T(2,128)S(1)} %get-tuple-element.7.force_ref), custom_call_target="tpu_custom_call" | custom-call | tf_op jit(solution)/shard_map/write_out/pallas_call | solution.py:635

commit v4 on v3

--- a/solution.py
+++ b/solution.py
@@ -80,26 +80,78 @@
 
 
 def flat(ref):
-    return ref.reshape(ref.shape[0], ref.shape[1] * ref.shape[2], ref.shape[3])
-
-
-def parts_of(whole, held):
-    parts = whole.shape[-1] // LANES
-    for t in range(whole.shape[-3]):
-        for q in range(parts):
-            yield whole.at[:, t, :, pl.ds(LANES * q, LANES)], held.at[:, parts * t + q]
-
-
-def write_out(phi_ref, force_ref, out_hbm, force_hbm, sem):
-    for n, (whole, held) in enumerate(((force_hbm, force_ref), (out_hbm, phi_ref))):
-        for dst, src in parts_of(whole, held):
-            pltpu.make_async_copy(src, dst, sem.at[n]).start()
-    for n, held in enumerate((force_ref, phi_ref)):
-        pltpu.make_async_copy(held, held, sem.at[n]).wait()
-
-
-def kernel(nt, nz, x_hbm, u_hbm, c_hbm, phi_out, force_out, psi_in, link_in, clov_in, hm, hp, bl,
-           sh_hm, sh_bl, prod, acc, hphi, sh_hphi, face_out, face_in, link_out, corner_in, in_sem,
+    return ref.reshape(ref.shape[0], ref.shape[1] * ref.shape[2] * ref.shape[3], ref.shape[4])
+
+
+def for_each(count, body, low=0):
+    def step(i, carry):
+        body(i)
+        return carry
+
+    lax.fori_loop(low, count, step, 0)
+
+
+def window(v):
+    return pl.ds(pl.multiple_of(v * TILE, TILE), TILE)
+
+
+def load_spinor(ref, at):
+    return [[(ref[3 * s + c, at, :], ref[12 + 3 * s + c, at, :]) for c in range(3)] for s in range(4)]
+
+
+def load_half(ref, mu, at):
+    return [[(ref[mu, 3 * s + c, at, :], ref[mu, 6 + 3 * s + c, at, :]) for c in range(3)] for s in range(2)]
+
+
+def load_link(ref, mu, at):
+    return [[(ref[18 * mu + 3 * a + b, at, :], ref[18 * mu + 9 + 3 * a + b, at, :]) for b in range(3)] for a in range(3)]
+
+
+def force_of(mu, v, phi, link, hp, prod, hphi, force_ref):
+    at = window(v)
+    zero = jnp.zeros((TILE, LANES), jnp.float32)
+    second = mat_vec(load_link(link, mu, at), load_half(hphi, mu, at), False)
+    second_right = load_half(hp, mu, at)
+    first = load_half(prod, mu, at)
+    first_right = half(mu, load_spinor(phi, at), -1.0)
+    pairs = [(first[s], first_right[s]) for s in range(2)] + [(second[s], second_right[s]) for s in range(2)]
+
+    def w_re(a, b):
+        return csum([l[a][0] * r[b][0] + l[a][1] * r[b][1] for l, r in pairs])
+
+    def w_im(a, b):
+        return csum([l[a][1] * r[b][0] - l[a][0] * r[b][1] for l, r in pairs])
+
+    diag = [w_im(a, a) for a in range(3)]
+    third = (diag[0] + diag[1] + diag[2]) * (1.0 / 3.0)
+    base = 18 * mu
+    for a in range(3):
+        force_ref[base + 4 * a, at, :] = zero
+        force_ref[base + 9 + 4 * a, at, :] = diag[a] - third
+        for b in range(a + 1, 3):
+            re = 0.5 * (w_re(a, b) - w_re(b, a))
+            im = 0.5 * (w_im(a, b) + w_im(b, a))
+            force_ref[base + 3 * a + b, at, :] = re
+            force_ref[base + 3 * b + a, at, :] = -re
+            force_ref[base + 9 + 3 * a + b, at, :] = im
+            force_ref[base + 9 + 3 * b + a, at, :] = im
+
+
+def finish_kernel(phi_in, early_in, link_in, hp, prod, hphi, phi_hbm, force_hbm, late, sem):
+    phi, link = flat(phi_in), flat(link_in)
+    count = early_in.shape[0]
+    pltpu.make_async_copy(early_in, force_hbm.at[pl.ds(0, count)], sem.at[0]).start()
+    pltpu.make_async_copy(phi_in, phi_hbm, sem.at[1]).start()
+    for mu in (3, 2):
+        for_each(phi.shape[1] // TILE, lambda v: force_of(mu, v, phi, link, hp, prod, hphi, flat(late)))
+        part = pl.ds(18 * mu, 18)
+        pltpu.make_async_copy(late.at[part], force_hbm.at[part], sem.at[0]).start()
+    pltpu.make_async_copy(phi_in, phi_hbm, sem.at[1]).wait()
+    pltpu.make_async_copy(late, force_hbm, sem.at[0]).wait()
+
+
+def kernel(nt, nz, x_hbm, u_hbm, c_hbm, phi_out, force_out, link_in, hp, prod, sh_hphi, psi_in, clov_in, hm, bl,
+           sh_hm, sh_bl, acc, hphi, face_out, face_in, link_out, corner_in, in_sem,
            send_sem, recv_sem, ready):
     psi, link, clov, out_ref, force_ref = map(flat, (psi_in, link_in, clov_in, phi_out, force_out))
     rows = psi.shape[1]
@@ -123,18 +175,15 @@
     barrier = pltpu.get_barrier_semaphore()
 
     groups = [(x_hbm, psi_in)]
-    for mu in range(4):
-        part = pl.ds(18 * mu, 18)
+    for part in (pl.ds(36, 18), pl.ds(54, 18), pl.ds(0, 36)):
         groups.append((u_hbm.at[part], link_in.at[part]))
     groups.append((c_hbm, clov_in))
 
     def fetch(n):
-        for src, dst in parts_of(*groups[n]):
-            pltpu.make_async_copy(src, dst, in_sem.at[n]).start()
+        pltpu.make_async_copy(*groups[n], in_sem.at[n]).start()
 
     def arrived(n):
-        held = groups[n][1]
-        pltpu.make_async_copy(held, held, in_sem.at[n]).wait()
+        pltpu.make_async_copy(*groups[n], in_sem.at[n]).wait()
 
     even = lax.rem(t_place, 2) == 0
     relay = jnp.logical_and(even, t_place > 0)
@@ -147,10 +196,11 @@
         def _():
             pl.semaphore_signal(barrier, inc=1, device_id=near[k], device_id_type=MESH)
 
+    after = {Z_PREV: relay, T_PREV: jnp.logical_and(t_place == 0, z_place == 1)}
     for k in range(4):
-        greet(k, jnp.logical_not(relay) if k == Z_PREV else True)
-
-    for n in (0, 3, 4):
+        greet(k, jnp.logical_not(after[k]) if k in after else True)
+
+    for n in (0, 1, 2):
         fetch(n)
     greeters = sum(f.astype(jnp.int32) for f in first)
 
@@ -158,19 +208,14 @@
     def _():
         pl.semaphore_wait(barrier, greeters)
 
-    greet(Z_PREV, relay)
+    for k, when in after.items():
+        greet(k, when)
     for k in range(4):
         @pl.when(first[k])
         def _():
             pl.semaphore_signal(ready.at[k ^ 1], inc=1, device_id=near[k], device_id_type=MESH)
-    for n in (1, 2, 5):
+    for n in (3, 4):
         fetch(n)
-
-    def window(v):
-        return pl.ds(pl.multiple_of(v * TILE, TILE), TILE)
-
-    def load_spinor(ref, at):
-        return [[(ref[3 * s + c, at, :], ref[12 + 3 * s + c, at, :]) for c in range(3)] for s in range(4)]
 
     def store_spinor(ref, at, value):
         for s in range(4):
@@ -178,17 +223,11 @@
                 ref[3 * s + c, at, :] = value[s][c][0]
                 ref[12 + 3 * s + c, at, :] = value[s][c][1]
 
-    def load_half(ref, mu, at):
-        return [[(ref[mu, 3 * s + c, at, :], ref[mu, 6 + 3 * s + c, at, :]) for c in range(3)] for s in range(2)]
-
     def store_half(ref, mu, at, value):
         for s in range(2):
             for c in range(3):
                 ref[mu, 3 * s + c, at, :] = value[s][c][0]
                 ref[mu, 6 + 3 * s + c, at, :] = value[s][c][1]
-
-    def load_link(mu, at):
-        return [[(link[18 * mu + 3 * a + b, at, :], link[18 * mu + 9 + 3 * a + b, at, :]) for b in range(3)] for a in range(3)]
 
     lane = lax.broadcasted_iota(jnp.int32, (rows, LANES), 1)
     row = lax.broadcasted_iota(jnp.int32, (rows, LANES), 0)
@@ -228,13 +267,6 @@
 
     def t_behind(src, dst, c):
         dst[3, c, pl.ds(face_t, rows - face_t), :] = src[3, c, pl.ds(0, rows - face_t), :]
-
-    def for_each(count, body, low=0):
-        def step(i, carry):
-            body(i)
-            return carry
-
-        lax.fori_loop(low, count, step, 0)
 
     t_last, z_last = nt - 1, nz - 1
     messages = {
@@ -271,20 +303,30 @@
                 k, held = place(name, i, c)
                 dst[mu, c, lines(at), :] = change(face_in[k, held, :], at, c)
 
+    together = ("a0", "b0", "c0", "d0", "a1 b1", "c1 d1", "e0 e1 f0 f1")
+    home = {name: n for n, some in enumerate(together) for name in some.split()}
+    sizes = {name: 12 * line * len(messages[name][1]) for name in names}
+
     def copy_of(name):
-        k, size = names.index(name), 12 * line * len(messages[name][1])
+        k, size = names.index(name), pl.ds(0, sizes[name])
         return pltpu.make_async_remote_copy(
-            src_ref=face_out.at[k, pl.ds(0, size)], dst_ref=face_in.at[k, pl.ds(0, size)], send_sem=send_sem.at[k],
-            recv_sem=recv_sem.at[k], device_id=near[messages[name][0]], device_id_type=MESH,
+            src_ref=face_out.at[k, size], dst_ref=face_in.at[k, size], send_sem=send_sem.at[0],
+            recv_sem=recv_sem.at[home[name]], device_id=near[messages[name][0]], device_id_type=MESH,
         )
 
     copies = {name: copy_of(name) for name in names}
+
+    def await_rows(count, sem):
+        held = face_in.reshape(face_in.shape[0] * face_in.shape[1], LANES).at[pl.ds(0, count)]
+        pltpu.make_async_copy(held, held, sem).wait()
+
+    CORNER = len(together)
 
     def corner_of(k, held, target):
         size = pl.ds(0, held.shape[0])
         return pltpu.make_async_remote_copy(
-            src_ref=held, dst_ref=corner_in.at[k, size], send_sem=send_sem.at[len(names) + k],
-            recv_sem=recv_sem.at[len(names) + k], device_id=target, device_id_type=MESH,
+            src_ref=held, dst_ref=corner_in.at[k, size], send_sem=send_sem.at[1],
+            recv_sem=recv_sem.at[CORNER], device_id=target, device_id_type=MESH,
         )
 
     t_before = near[T_PREV][0]
@@ -292,7 +334,11 @@
         corner_of(0, face_out.at[names.index("d0"), pl.ds(0, 12 * line)], (t_before, near[Z_NEXT][1])),
         corner_of(1, face_out.at[names.index("c0"), pl.ds(0, 12 * line)], (t_before, near[Z_PREV][1])),
         corner_of(2, link_out, near[T_PREV]),
+        corner_of(0, face_out.at[names.index("b0"), pl.ds(0, 12 * line)], (near[T_NEXT][0], near[Z_PREV][1])),
     ]
+    edge = jnp.logical_and(t_place == 0, z_place == 1)
+    edge_from = jnp.logical_and(t_place == t_count - 1, z_place == 1)
+    edge_to = jnp.logical_and(t_place == 0, z_low)
     relay_high, relay_low = jnp.logical_and(relay, z_high), jnp.logical_and(relay, z_low)
     relayed_high, relayed_low = jnp.logical_and(relayed, z_high), jnp.logical_and(relayed, z_low)
     def sender(mine):
@@ -320,8 +366,8 @@
     odd_early, odd_late = sender(jnp.logical_not(even))
 
     def received(*some):
-        for name in some:
-            copies[name].wait_recv()
+        assert set(some) == {name for name in names if home[name] == home[some[0]]}
+        await_rows(sum(sizes[name] for name in some), recv_sem.at[home[some[0]]])
 
     def project(mu, v):
         at = window(v)
@@ -329,7 +375,7 @@
         store_half(hm, mu, at, half(mu, field, -1.0))
         ahead = half(mu, field, 1.0)
         store_half(hp, mu, at, ahead)
-        store_half(bl, mu, at, mat_vec(load_link(mu, at), ahead, True))
+        store_half(bl, mu, at, mat_vec(load_link(link, mu, at), ahead, True))
 
     def behind(v):
         at = window(v)
@@ -342,7 +388,7 @@
         pack(name, hm, 2)
     for name in ("c0", "c1"):
         pl.when(jnp.logical_and(inner, first[Z_PREV]))(copies[name].start)
-    arrived(3)
+    arrived(1)
     for_each(chunks, lambda v: project(2, v))
     for name in ("d0", "d1"):
         pack(name, bl, 2)
@@ -352,7 +398,7 @@
         pl.when(relay_high)(copies[name].start)
     for name in ("d1", "c0"):
         pl.when(jnp.logical_and(z_high, t_place == 0))(copies[name].start)
-    arrived(4)
+    arrived(2)
     for_each(chunks, lambda v: project(3, v))
     for name in ("a0", "a1"):
         pack(name, hm, 3)
@@ -360,6 +406,7 @@
         pack(name, bl, 3)
     even_early("b0", "a0", "a1", "b1")
     even_late("b0", "b1")
+    pl.when(edge_from)(corners[3].start)
     odd_early("a0", "b0", "a1", "b1", "d0")
     for c in range(18):
         link_out[c * line:(c + 1) * line, :] = link[36 + c, lines((0, z_last)), :]
@@ -367,9 +414,8 @@
     pl.when(jnp.logical_and(even, z_high))(copies["c1"].start)
     pl.when(jnp.logical_and(jnp.logical_not(even), z_high))(copies["c0"].start)
 
-    arrived(1)
+    arrived(3)
     for_each(chunks, lambda v: project(0, v))
-    arrived(2)
     for_each(chunks, lambda v: project(1, v))
 
     for c in range(12):
@@ -383,7 +429,7 @@
         t_behind(bl, sh_bl, c)
 
     def hop(mu, at, total):
-        ahead = mat_vec(load_link(mu, at), load_half(sh_hm, mu, at), False)
+        ahead = mat_vec(load_link(link, mu, at), load_half(sh_hm, mu, at), False)
         store_half(prod, mu, at, ahead)
         total = add_whole(mu, total, ahead, -1.0)
         return add_whole(mu, total, load_half(sh_bl, mu, at), 1.0)
@@ -395,7 +441,7 @@
 
     even_late("d0", "d1")
     odd_late("d0", "d1")
-    arrived(5)
+    arrived(4)
 
     def local(v):
         at = window(v)
@@ -464,16 +510,31 @@
     even_late("a0", "a1")
     odd_late("a0", "a1")
 
-    received("a0")
-    unpack("a0", sh_hm, 3, signed(high_sign))
-    for_each(chunks, lambda v: partial(3, 2, v), high_chunk)
-    pack("e1", hphi, 2)
-    copies["e1"].start()
-    received("b0")
-    unpack("b0", sh_bl, 3, signed(low_sign))
-    for_each(-(-(rows - face_t) // TILE), lambda v: partial(3, 2, v))
-    pack("e0", hphi, 2)
-    copies["e0"].start()
+    def send_e(name):
+        low, high = (high_chunk, chunks) if name == "e1" else (0, -(-(rows - face_t) // TILE))
+        for_each(high, lambda v: partial(3, 2, v), low)
+        pack(name, hphi, 2)
+        copies[name].start()
+
+    def take_a():
+        received("a0")
+        unpack("a0", sh_hm, 3, signed(high_sign))
+        send_e("e1")
+
+    def take_b():
+        received("b0")
+        unpack("b0", sh_bl, 3, signed(low_sign))
+        pl.when(jnp.logical_not(edge))(lambda: send_e("e0"))
+
+    @pl.when(edge)
+    def _():
+        for c in range(12):
+            sh_bl[3, c, lines((0, 0)), :] = jnp.zeros((line, LANES), jnp.float32)
+        send_e("e0")
+
+    pl.when(jnp.logical_not(even))(take_b)
+    take_a()
+    pl.when(even)(take_b)
 
     def take_c():
         received("c0")
@@ -517,40 +578,14 @@
         z_ahead(hphi, sh_hphi, c)
         t_ahead(hphi, sh_hphi, c)
 
-    def force(mu, v):
-        at = window(v)
-        second = mat_vec(load_link(mu, at), load_half(sh_hphi, mu, at), False)
-        second_right = load_half(hp, mu, at)
-        first = load_half(prod, mu, at)
-        first_right = half(mu, load_spinor(out_ref, at), -1.0)
-        pairs = [(first[s], first_right[s]) for s in range(2)] + [(second[s], second_right[s]) for s in range(2)]
-
-        def w_re(a, b):
-            return csum([l[a][0] * r[b][0] + l[a][1] * r[b][1] for l, r in pairs])
-
-        def w_im(a, b):
-            return csum([l[a][1] * r[b][0] - l[a][0] * r[b][1] for l, r in pairs])
-
-        diag = [w_im(a, a) for a in range(3)]
-        third = (diag[0] + diag[1] + diag[2]) * (1.0 / 3.0)
-        base = 18 * mu
-        for a in range(3):
-            force_ref[base + 4 * a, at, :] = zero
-            force_ref[base + 9 + 4 * a, at, :] = diag[a] - third
-            for b in range(a + 1, 3):
-                re = 0.5 * (w_re(a, b) - w_re(b, a))
-                im = 0.5 * (w_im(a, b) + w_im(b, a))
-                force_ref[base + 3 * a + b, at, :] = re
-                force_ref[base + 3 * b + a, at, :] = -re
-                force_ref[base + 9 + 3 * a + b, at, :] = im
-                force_ref[base + 9 + 3 * b + a, at, :] = im
-
     for mu in (0, 1):
-        for_each(chunks, lambda v: force(mu, v))
-
+        for_each(chunks, lambda v: force_of(mu, v, out_ref, link, hp, prod, sh_hphi, force_ref))
+
+    received("e0", "e1", "f0", "f1")
     for name in ("f0", "f1"):
-        received(name)
         unpack(name, sh_hphi, 3, lambda value, at, c: value * high_sign - bl[3, c, lines(at), :])
+    for name in ("e0", "e1"):
+        unpack(name, sh_hphi, 2, lambda value, at, c: value - bl[2, c, lines(at), :])
 
     def corner(k, c):
         return corner_in[k, c * line:(c + 1) * line, :]
@@ -560,43 +595,47 @@
 
     none = [[(0.0, 0.0)] * 3 for _ in range(4)]
 
-    def add_corner(value, sign, z):
-        extra = half(3, add_whole(2, none, value, sign), 1.0)
+    def add_corner(across, along, value, sign, at, factor):
+        extra = half(along, add_whole(across, none, value, sign), 1.0)
         for s in range(2):
             for c in range(3):
                 for n, part in enumerate(extra[s][c]):
-                    place = 3, 6 * n + 3 * s + c, lines((t_last, z)), slice(None)
-                    sh_hphi[place] = sh_hphi[place] - 0.5 * high_sign * part
+                    place = along, 6 * n + 3 * s + c, lines(at), slice(None)
+                    sh_hphi[place] = sh_hphi[place] - 0.5 * factor * part
 
     @pl.when(relayed_low)
     def _():
-        corners[0].wait_recv()
-        add_corner(corner_half(0), 1.0, 0)
+        await_rows(12 * line, recv_sem.at[CORNER])
+        add_corner(2, 3, corner_half(0), 1.0, (t_last, 0), high_sign)
 
     @pl.when(relayed_high)
     def _():
-        corners[2].wait_recv()
-        corners[1].wait_recv()
+        await_rows(30 * line, recv_sem.at[CORNER])
         near_link = [[(corner(2, 3 * a + b), corner(2, 9 + 3 * a + b)) for b in range(3)] for a in range(3)]
-        add_corner(mat_vec(near_link, corner_half(1), False), -1.0, z_last)
-
-    for_each(chunks, lambda v: force(3, v))
-    for name in ("e0", "e1"):
-        received(name)
-        unpack(name, sh_hphi, 2, lambda value, at, c: value - bl[2, c, lines(at), :])
-    for_each(chunks, lambda v: force(2, v))
-    for name in names:
-        copies[name].wait_send()
-    for k, mine in enumerate((relay_high, relay_low, relay_high)):
-        pl.when(mine)(corners[k].wait_send)
+        add_corner(2, 3, mat_vec(near_link, corner_half(1), False), -1.0, (t_last, z_last), high_sign)
+
+    @pl.when(edge_to)
+    def _():
+        await_rows(12 * line, recv_sem.at[CORNER])
+        add_corner(3, 2, corner_half(0), 1.0, (0, z_last), low_sign)
+
+    await_rows(sum(sizes.values()), send_sem.at[0])
+    for mine, count in ((relay_high, 30), (jnp.logical_or(relay_low, edge_from), 12)):
+        pl.when(mine)(lambda: await_rows(count * line, send_sem.at[1]))
 
 
 def body(spinor, links, clover):
-    nt, nz = spinor.shape[3], spinor.shape[4]
-    sites = spinor.shape[-3:]
-    x, u, c = (a.reshape((-1,) + sites) for a in (spinor, links, clover))
-    parts = nt * (sites[2] // LANES)
-    rows = parts * nz
+    nt, nz, plane = spinor.shape[-3:]
+    pieces = plane // LANES
+
+    def tiled(a):
+        return a.reshape(-1, nt, nz, pieces, LANES).transpose(0, 1, 3, 2, 4)
+
+    def untiled(a, shape):
+        return a.transpose(0, 1, 3, 2, 4).reshape(shape)
+
+    x, u, c = map(tiled, (spinor, links, clover))
+    rows = nt * pieces * nz
     assert nt > 1 and nz > 1
     line = rows // (nt * nz)
     face = max(nt - 1, nz - 1) * line
@@ -605,46 +644,45 @@
         return pltpu.VMEM((4, 12, rows, LANES), jnp.float32)
 
     def held(array):
-        return pltpu.VMEM((array.shape[0], parts, nz, LANES), jnp.float32)
-
-    phi, anti = pl.pallas_call(
+        return pltpu.VMEM(array.shape, jnp.float32)
+
+    made = pl.pallas_call(
         lambda *refs: kernel(nt, nz, *refs),
         name="wilson",
-        out_shape=(
-            pltpu.VMEM((24, parts, nz, LANES), jnp.float32),
-            pltpu.VMEM((u.shape[0], parts, nz, LANES), jnp.float32),
-        ),
+        out_shape=(held(x), held(u[:36]), held(u), halves(), halves(), halves()),
         in_specs=[pl.BlockSpec(memory_space=pltpu.HBM)] * 3,
-        out_specs=(pl.BlockSpec(memory_space=pltpu.VMEM),) * 2,
+        out_specs=(pl.BlockSpec(memory_space=pltpu.VMEM),) * 6,
         scratch_shapes=[
-            held(x), held(u), held(c),
-            halves(), halves(), halves(), halves(), halves(), halves(),
+            held(x), held(c),
+            halves(), halves(), halves(), halves(),
             pltpu.VMEM((24, rows, LANES), jnp.float32),
-            halves(), halves(),
+            halves(),
             pltpu.VMEM((12, 12 * face, LANES), jnp.float32),
             pltpu.VMEM((12, 12 * face, LANES), jnp.float32),
             pltpu.VMEM((18 * line, LANES), jnp.float32),
             pltpu.VMEM((3, 18 * line, LANES), jnp.float32),
-            pltpu.SemaphoreType.DMA((6,)),
-            pltpu.SemaphoreType.DMA((15,)),
-            pltpu.SemaphoreType.DMA((15,)),
+            pltpu.SemaphoreType.DMA((5,)),
+            pltpu.SemaphoreType.DMA((2,)),
+            pltpu.SemaphoreType.DMA((8,)),
             pltpu.SemaphoreType.REGULAR((4,)),
         ],
-        compiler_params=pltpu.CompilerParams(collective_id=0, has_side_effects=True, vmem_limit_bytes=56 * 1024 * 1024),
+        compiler_params=pltpu.CompilerParams(
+            collective_id=0, has_side_effects=True, vmem_limit_bytes=54 * 1024 * 1024
+        ),
     )(x, u, c)
     applied, force = pl.pallas_call(
-        write_out,
-        name="write_out",
+        finish_kernel,
+        name="finish",
         out_shape=(
             jax.ShapeDtypeStruct(x.shape, jnp.float32),
             jax.ShapeDtypeStruct(u.shape, jnp.float32),
         ),
-        in_specs=[pl.BlockSpec(memory_space=pltpu.VMEM)] * 2,
+        in_specs=[pl.BlockSpec(memory_space=pltpu.VMEM)] * 6,
         out_specs=(pl.BlockSpec(memory_space=pl.ANY),) * 2,
-        scratch_shapes=[pltpu.SemaphoreType.DMA((2,))],
+        scratch_shapes=[held(u), pltpu.SemaphoreType.DMA((2,))],
         compiler_params=pltpu.CompilerParams(vmem_limit_bytes=8 * 1024 * 1024),
-    )(phi, anti)
-    return applied.reshape(spinor.shape), force.reshape(links.shape)
+    )(*made)
+    return untiled(applied, spinor.shape), untiled(force, links.shape)
 
 
 def solution(mesh):

time: 12.7 us -> 12.1 us (0.953)
  Pallas kernels: 11.9 us -> 11.3 us
    pallas_call x1, Pallas kernels: 10.9 us -> 10.2 us  [body(): pl.pallas_call(lambda *refs: kernel(nt, nz, *refs), name='wilson', out_sh...]
where the time goes in v4:
time: 12.1 us; the launch traced here: 11.9 us
  Pallas kernels  11.3 us (93%)
  between operations  0.64 us (5%)
    pallas_call x1, Pallas kernels, body(): pl.pallas_call(lambda *refs: kernel(nt, nz, *refs), name='wilson', out_sh...  10.2 us
    pallas_call x1, Pallas kernels, body(): pl.pallas_call(finish_kernel, name='finish', out_shape=(jax.ShapeDtypeStr...  1.07 us

profile of v4, /device:TPU:0, one launch (start us, length us, event | category | flops | bytes accessed | tf_op | source)
XLA Modules:
  0.0 11.9 jit_solution(180691262255836701)
XLA Ops:
  0.6 10.2 %wilson.1 = (f32[24,2,6,2,128]{4,3,2,1,0:T(2,128)S(1)}, f32[36,2,6,2,128]{4,3,2,1,0:T(2,128)S(1)}, f32[72,2,6,2,128]{4,3,2,1,0:T(2,128)S(1)}, f32[4,12,24,128]{3...) custom-call(f32[24,2,6,2,128]{4,3,2,1,0:T(2,128)} %bitcast.17, ...), custom_call_target="tpu_custom_call" | custom-call | tf_op jit(solution)/shard_map/wilson/pallas_call | solution.py:649
  10.9 1.1 %finish.1 = (f32[24,2,6,2,128]{4,3,2,1,0:T(2,128)}, f32[72,2,6,2,128]{4,3,2,1,0:T(2,128)}) custom-call(f32[24,2,6,2,128]{4,3,2,1,0:T(2,128)S(1)} %get-tuple-element.10.phi_in, f32[36,2,6,2,128]{4,3,2,1,0:T(2,128)S(1)} %get-tuple-element.11.early_in, f32[72,2,6,2,128]{4,3,2,1,0:T(2,128)S(1)} %get-tuple-element.12.link_in, ...), custom_call_target="tpu_custom_call" | custom-call | tf_op jit(solution)/shard_map/finish/pallas_call | solution.py:673

commit v5 on v4

--- a/solution.py
+++ b/solution.py
@@ -107,7 +107,7 @@
     return [[(ref[18 * mu + 3 * a + b, at, :], ref[18 * mu + 9 + 3 * a + b, at, :]) for b in range(3)] for a in range(3)]
 
 
-def force_of(mu, v, phi, link, hp, prod, hphi, force_ref):
+def force_of(mu, v, phi, link, hp, prod, hphi, force_ref, base):
     at = window(v)
     zero = jnp.zeros((TILE, LANES), jnp.float32)
     second = mat_vec(load_link(link, mu, at), load_half(hphi, mu, at), False)
@@ -124,7 +124,6 @@
 
     diag = [w_im(a, a) for a in range(3)]
     third = (diag[0] + diag[1] + diag[2]) * (1.0 / 3.0)
-    base = 18 * mu
     for a in range(3):
         force_ref[base + 4 * a, at, :] = zero
         force_ref[base + 9 + 4 * a, at, :] = diag[a] - third
@@ -139,15 +138,25 @@
 
 def finish_kernel(phi_in, early_in, link_in, hp, prod, hphi, phi_hbm, force_hbm, late, sem):
     phi, link = flat(phi_in), flat(link_in)
-    count = early_in.shape[0]
-    pltpu.make_async_copy(early_in, force_hbm.at[pl.ds(0, count)], sem.at[0]).start()
-    pltpu.make_async_copy(phi_in, phi_hbm, sem.at[1]).start()
-    for mu in (3, 2):
-        for_each(phi.shape[1] // TILE, lambda v: force_of(mu, v, phi, link, hp, prod, hphi, flat(late)))
-        part = pl.ds(18 * mu, 18)
-        pltpu.make_async_copy(late.at[part], force_hbm.at[part], sem.at[0]).start()
-    pltpu.make_async_copy(phi_in, phi_hbm, sem.at[1]).wait()
-    pltpu.make_async_copy(late, force_hbm, sem.at[0]).wait()
+    corner = jnp.logical_and(lax.axis_index("ta") == 0, lax.axis_index("gz") == 0)
+
+    def write(held, mu, count=1):
+        pltpu.make_async_copy(held, force_hbm.at[pl.ds(18 * mu, 18 * count)], sem.at[0]).start()
+
+    def compute(mu, base):
+        for_each(
+            phi.shape[1] // TILE, lambda v: force_of(mu, v, phi, link, hp, prod, hphi, flat(late), base)
+        )
+        write(late.at[pl.ds(base, 18)], mu)
+
+    write(early_in.at[pl.ds(0, 36)], 0, 2)
+    applied = pltpu.make_async_copy(phi_in, phi_hbm, sem.at[1])
+    applied.start()
+    pl.when(corner)(lambda: write(early_in.at[pl.ds(36, 18)], 3))
+    pl.when(jnp.logical_not(corner))(lambda: compute(3, 18))
+    compute(2, 0)
+    applied.wait()
+    pltpu.make_async_copy(force_hbm, force_hbm, sem.at[0]).wait()
 
 
 def kernel(nt, nz, x_hbm, u_hbm, c_hbm, phi_out, force_out, link_in, hp, prod, sh_hphi, psi_in, clov_in, hm, bl,
@@ -196,11 +205,12 @@
         def _():
             pl.semaphore_signal(barrier, inc=1, device_id=near[k], device_id_type=MESH)
 
+    fetch(0)
     after = {Z_PREV: relay, T_PREV: jnp.logical_and(t_place == 0, z_place == 1)}
     for k in range(4):
         greet(k, jnp.logical_not(after[k]) if k in after else True)
 
-    for n in (0, 1, 2):
+    for n in (1, 2):
         fetch(n)
     greeters = sum(f.astype(jnp.int32) for f in first)
 
@@ -303,7 +313,7 @@
                 k, held = place(name, i, c)
                 dst[mu, c, lines(at), :] = change(face_in[k, held, :], at, c)
 
-    together = ("a0", "b0", "c0", "d0", "a1 b1", "c1 d1", "e0 e1 f0 f1")
+    together = ("a0", "b0", "c0", "d0", "a1 b1", "c1 d1", "e0 e1", "f0 f1")
     home = {name: n for n, some in enumerate(together) for name in some.split()}
     sizes = {name: 12 * line * len(messages[name][1]) for name in names}
 
@@ -377,26 +387,23 @@
         store_half(hp, mu, at, ahead)
         store_half(bl, mu, at, mat_vec(load_link(link, mu, at), ahead, True))
 
-    def behind(v):
-        at = window(v)
-        store_half(hm, 2, at, half(2, load_spinor(psi, at), -1.0))
-
     inner = jnp.logical_not(first[Z_NEXT])
     arrived(0)
-    for_each(chunks, behind)
     for name in ("c0", "c1"):
-        pack(name, hm, 2)
+        for i, at in enumerate(messages[name][1]):
+            ahead = half(2, load_spinor(psi, lines(at)), -1.0)
+            for c in range(12):
+                k, spot = place(name, i, c)
+                face_out[k, spot, :] = ahead[c % 6 // 3][c % 3][c // 6]
     for name in ("c0", "c1"):
         pl.when(jnp.logical_and(inner, first[Z_PREV]))(copies[name].start)
     arrived(1)
     for_each(chunks, lambda v: project(2, v))
     for name in ("d0", "d1"):
         pack(name, bl, 2)
-    pl.when(relay_high)(corners[0].start)
-    even_early("d0")
-    for name in ("c0", "d1"):
-        pl.when(relay_high)(copies[name].start)
-    for name in ("d1", "c0"):
+    for some in (copies["c0"], corners[0], copies["d0"], copies["d1"]):
+        pl.when(relay_high)(some.start)
+    for name in ("d0", "d1", "c0"):
         pl.when(jnp.logical_and(z_high, t_place == 0))(copies[name].start)
     arrived(2)
     for_each(chunks, lambda v: project(3, v))
@@ -500,12 +507,15 @@
     send_f("f0", relay_low)
     send_f("f1", relay_high)
 
-    @pl.when(jnp.logical_and(z_low, True))
+    def wrap():
+        copies["c0"].start()
+        copies["c1"].start()
+
+    @pl.when(z_low)
     def _():
         pl.semaphore_wait(ready.at[Z_PREV], 1)
         pl.when(relay)(corners[1].start)
-        copies["c0"].start()
-        copies["c1"].start()
+        pl.when(jnp.logical_not(relayed))(wrap)
 
     even_late("a0", "a1")
     odd_late("a0", "a1")
@@ -535,6 +545,7 @@
     pl.when(jnp.logical_not(even))(take_b)
     take_a()
     pl.when(even)(take_b)
+    pl.when(jnp.logical_and(z_low, relayed))(wrap)
 
     def take_c():
         received("c0")
@@ -579,11 +590,17 @@
         t_ahead(hphi, sh_hphi, c)
 
     for mu in (0, 1):
-        for_each(chunks, lambda v: force_of(mu, v, out_ref, link, hp, prod, sh_hphi, force_ref))
-
-    received("e0", "e1", "f0", "f1")
+        for_each(chunks, lambda v: force_of(mu, v, out_ref, link, hp, prod, sh_hphi, force_ref, 18 * mu))
+
+    received("f0", "f1")
     for name in ("f0", "f1"):
         unpack(name, sh_hphi, 3, lambda value, at, c: value * high_sign - bl[3, c, lines(at), :])
+
+    @pl.when(edge_to)
+    def _():
+        for_each(chunks, lambda v: force_of(3, v, out_ref, link, hp, prod, sh_hphi, force_ref, 36))
+
+    received("e0", "e1")
     for name in ("e0", "e1"):
         unpack(name, sh_hphi, 2, lambda value, at, c: value - bl[2, c, lines(at), :])
 
@@ -649,7 +666,7 @@
     made = pl.pallas_call(
         lambda *refs: kernel(nt, nz, *refs),
         name="wilson",
-        out_shape=(held(x), held(u[:36]), held(u), halves(), halves(), halves()),
+        out_shape=(held(x), held(u[:54]), held(u), halves(), halves(), halves()),
         in_specs=[pl.BlockSpec(memory_space=pltpu.HBM)] * 3,
         out_specs=(pl.BlockSpec(memory_space=pltpu.VMEM),) * 6,
         scratch_shapes=[
@@ -663,7 +680,7 @@
             pltpu.VMEM((3, 18 * line, LANES), jnp.float32),
             pltpu.SemaphoreType.DMA((5,)),
             pltpu.SemaphoreType.DMA((2,)),
-            pltpu.SemaphoreType.DMA((8,)),
+            pltpu.SemaphoreType.DMA((9,)),
             pltpu.SemaphoreType.REGULAR((4,)),
         ],
         compiler_params=pltpu.CompilerParams(
@@ -679,7 +696,7 @@
         ),
         in_specs=[pl.BlockSpec(memory_space=pltpu.VMEM)] * 6,
         out_specs=(pl.BlockSpec(memory_space=pl.ANY),) * 2,
-        scratch_shapes=[held(u), pltpu.SemaphoreType.DMA((2,))],
+        scratch_shapes=[held(u[:36]), pltpu.SemaphoreType.DMA((2,))],
         compiler_params=pltpu.CompilerParams(vmem_limit_bytes=8 * 1024 * 1024),
     )(*made)
     return untiled(applied, spinor.shape), untiled(force, links.shape)

time: 12.1 us -> 12 us (level)
  no operation moved by 1% of the time
where the time goes in v5:
time: 12 us; the launch traced here: 11.9 us
  Pallas kernels  11.2 us (93%)
  between operations  0.64 us (5%)
    pallas_call x1, Pallas kernels, body(): pl.pallas_call(lambda *refs: kernel(nt, nz, *refs), name='wilson', out_sh...  10.2 us
    pallas_call x1, Pallas kernels, body(): pl.pallas_call(finish_kernel, name='finish', out_shape=(jax.ShapeDtypeStr...  1.02 us

profile of v5, /device:TPU:0, one launch (start us, length us, event | category | flops | bytes accessed | tf_op | source)
XLA Modules:
  0.0 11.9 jit_solution(9403770223600589417)
XLA Ops:
  0.6 10.2 %wilson.1 = (f32[24,2,6,2,128]{4,3,2,1,0:T(2,128)S(1)}, f32[54,2,6,2,128]{4,3,2,1,0:T(2,128)S(1)}, f32[72,2,6,2,128]{4,3,2,1,0:T(2,128)S(1)}, f32[4,12,24,128]{3...) custom-call(f32[24,2,6,2,128]{4,3,2,1,0:T(2,128)} %bitcast.17, ...), custom_call_target="tpu_custom_call" | custom-call | tf_op jit(solution)/shard_map/wilson/pallas_call | solution.py:666
  10.8 1.0 %finish.1 = (f32[24,2,6,2,128]{4,3,2,1,0:T(2,128)}, f32[72,2,6,2,128]{4,3,2,1,0:T(2,128)}) custom-call(f32[24,2,6,2,128]{4,3,2,1,0:T(2,128)S(1)} %get-tuple-element.10.phi_in, f32[54,2,6,2,128]{4,3,2,1,0:T(2,128)S(1)} %get-tuple-element.11.early_in, f32[72,2,6,2,128]{4,3,2,1,0:T(2,128)S(1)} %get-tuple-element.12.link_in, ...), custom_call_target="tpu_custom_call" | custom-call | tf_op jit(solution)/shard_map/finish/pallas_call | solution.py:690

commit v6 on v5

--- a/solution.py
+++ b/solution.py
@@ -184,7 +184,7 @@
     barrier = pltpu.get_barrier_semaphore()
 
     groups = [(x_hbm, psi_in)]
-    for part in (pl.ds(36, 18), pl.ds(54, 18), pl.ds(0, 36)):
+    for part in (pl.ds(36, 36), pl.ds(0, 36)):
         groups.append((u_hbm.at[part], link_in.at[part]))
     groups.append((c_hbm, clov_in))
 
@@ -210,8 +210,7 @@
     for k in range(4):
         greet(k, jnp.logical_not(after[k]) if k in after else True)
 
-    for n in (1, 2):
-        fetch(n)
+    fetch(1)
     greeters = sum(f.astype(jnp.int32) for f in first)
 
     @pl.when(greeters > 0)
@@ -224,7 +223,7 @@
         @pl.when(first[k])
         def _():
             pl.semaphore_signal(ready.at[k ^ 1], inc=1, device_id=near[k], device_id_type=MESH)
-    for n in (3, 4):
+    for n in (2, 3):
         fetch(n)
 
     def store_spinor(ref, at, value):
@@ -405,7 +404,6 @@
         pl.when(relay_high)(some.start)
     for name in ("d0", "d1", "c0"):
         pl.when(jnp.logical_and(z_high, t_place == 0))(copies[name].start)
-    arrived(2)
     for_each(chunks, lambda v: project(3, v))
     for name in ("a0", "a1"):
         pack(name, hm, 3)
@@ -421,7 +419,7 @@
     pl.when(jnp.logical_and(even, z_high))(copies["c1"].start)
     pl.when(jnp.logical_and(jnp.logical_not(even), z_high))(copies["c0"].start)
 
-    arrived(3)
+    arrived(2)
     for_each(chunks, lambda v: project(0, v))
     for_each(chunks, lambda v: project(1, v))
 
@@ -448,7 +446,7 @@
 
     even_late("d0", "d1")
     odd_late("d0", "d1")
-    arrived(4)
+    arrived(3)
 
     def local(v):
         at = window(v)
@@ -678,7 +676,7 @@
             pltpu.VMEM((12, 12 * face, LANES), jnp.float32),
             pltpu.VMEM((18 * line, LANES), jnp.float32),
             pltpu.VMEM((3, 18 * line, LANES), jnp.float32),
-            pltpu.SemaphoreType.DMA((5,)),
+            pltpu.SemaphoreType.DMA((4,)),
             pltpu.SemaphoreType.DMA((2,)),
             pltpu.SemaphoreType.DMA((9,)),
             pltpu.SemaphoreType.REGULAR((4,)),

time: 12 us -> 12.1 us (level)
  no operation moved by 1% of the time
where the time goes in v6:
time: 12.1 us; the launch traced here: 11.9 us
  Pallas kernels  11.3 us (93%)
  between operations  0.64 us (5%)
    pallas_call x1, Pallas kernels, body(): pl.pallas_call(lambda *refs: kernel(nt, nz, *refs), name='wilson', out_sh...  10.3 us
    pallas_call x1, Pallas kernels, body(): pl.pallas_call(finish_kernel, name='finish', out_shape=(jax.ShapeDtypeStr...  1.02 us

profile of v6, /device:TPU:0, one launch (start us, length us, event | category | flops | bytes accessed | tf_op | source)
XLA Modules:
  0.0 11.9 jit_solution(6119221829210975581)
XLA Ops:
  0.6 10.3 %wilson.1 = (f32[24,2,6,2,128]{4,3,2,1,0:T(2,128)S(1)}, f32[54,2,6,2,128]{4,3,2,1,0:T(2,128)S(1)}, f32[72,2,6,2,128]{4,3,2,1,0:T(2,128)S(1)}, f32[4,12,24,128]{3...) custom-call(f32[24,2,6,2,128]{4,3,2,1,0:T(2,128)} %bitcast.17, ...), custom_call_target="tpu_custom_call" | custom-call | tf_op jit(solution)/shard_map/wilson/pallas_call | solution.py:664
  10.9 1.0 %finish.1 = (f32[24,2,6,2,128]{4,3,2,1,0:T(2,128)}, f32[72,2,6,2,128]{4,3,2,1,0:T(2,128)}) custom-call(f32[24,2,6,2,128]{4,3,2,1,0:T(2,128)S(1)} %get-tuple-element.10.phi_in, f32[54,2,6,2,128]{4,3,2,1,0:T(2,128)S(1)} %get-tuple-element.11.early_in, f32[72,2,6,2,128]{4,3,2,1,0:T(2,128)S(1)} %get-tuple-element.12.link_in, ...), custom_call_target="tpu_custom_call" | custom-call | tf_op jit(solution)/shard_map/finish/pallas_call | solution.py:688
